TPU v7x, 128 devices: a whole 4x4x4 slice. The times are simulated.
128 devices in a mesh: flow: 32 (over y, x, core), chem: 4 (over z).
Axes of the slice: x: 4, y: 4, z: 4, core: 2. Of those that a mesh axis runs over, the one named last changes fastest.
Arguments:
- component_levels: float32 [2048, 111, 512], P('flow', None, 'chem'), may hold values from 0.1 to 2
- thermal_field: float32 [2048, 512], P('flow', 'chem'), may hold values from 0.5 to 2.7
- reciprocal_pair_diffusivity: float32 [111, 111], replicated, may hold values from 0.005 to 0.02
- log_arrhenius_factor: float32 [784], replicated, may hold values from -1 to 6
- kinetic_exponents: float32 [784, 111], replicated, may hold values from 0 to 0.05
- arrhenius_energies: float32 [784], replicated, may hold values from 0.5 to 4
- molar_change_matrix: float32 [111, 784], replicated, may hold values from -0.21875 to 0.21875
- cooling_by_component: float32 [111], replicated, may hold values from -1 to 1
- burning_flags: int32 [2048, 4], P('flow', 'chem'), may hold values from 0 to 1, as said below
Outputs:
- advanced_components: float32 [2048, 111, 512], P('flow', None, 'chem')
- advanced_thermal: float32 [2048, 512], P('flow', 'chem')
Inputs may be any that keep to these rules, and one draw needn't show every extreme that they name: `burning_flags`: each device's 64 rows hold at most 24 reacting blocks, and at least one device of every chem index holds exactly 24; the devices of one chem index hold exactly 256 reacting blocks together.
All inputs are finite; a program needn't handle non-finite values.
Results may differ from a plain program's by a relative error of at most 0.000058.
Values sent between devices are 32-bit elements; how exact they have to be, the bound alone decides.
No kernel may reach another device: no remote copies, remote signals or barrier semaphores. Data moves between devices by JAX's collectives and lax.ppermute only.
A program may use at most 192 MiB of HBM per device.

v0:
```python
import functools

import jax
import jax.numpy as jnp
from jax import lax
from jax.experimental import pallas as pl
from jax.experimental.pallas import tpu as pltpu
from jax.sharding import Mesh
from jax.sharding import PartitionSpec as P

FLOW = ("flow_0", "flow_1", "flow_2")
FLOW_CHEM = ("flow_0", "flow_1", "flow_2", "chem")

COURANT = 0.2
CHEM_STEP = 0.05
LOG_OFFSET = 0.001
RATE_CEILING = 2.0
LOG2E = 1.4426950408889634

F32 = jnp.float32
BF16 = jnp.bfloat16
LANES = 128
GROUP = 4
CHUNK = 8


def split2(value):
    high = value.astype(BF16)
    return high, (value - high.astype(F32)).astype(BF16)


def split3(value):
    high = value.astype(BF16)
    rest = value - high.astype(F32)
    mid = rest.astype(BF16)
    return high, mid, (rest - mid.astype(F32)).astype(BF16)


def mxu(lhs, rhs):
    return jnp.dot(lhs, rhs, preferred_element_type=F32)


def mixture(cells, stacked):
    padded = cells.shape[0]
    high, low = split2(cells)
    both = mxu(stacked[...], high)
    total = both[:padded] + both[padded:] + mxu(stacked[0:padded], low)
    heat = cells[padded - 1 : padded]
    there = heat > 0.0
    scaled = heat * jnp.sqrt(heat)
    return jnp.where(there, scaled, 0.0) / jnp.where(there, total, 1.0)


def lane_index(shape):
    return lax.broadcasted_iota(jnp.int32, shape, len(shape) - 1)


def spread_kernel(
    species, reactions, x_ref, t_ref, r_ref, a_ref, k_ref, e_ref, m_ref,
    c_ref, d_ref, top_ref, bottom_ref, cols_ref, peak_ref, rs_ref, ka_ref, ms_ref,
    square, rows, tall, wide,
):
    padded = c_ref.shape[1]
    step = pl.program_id(0)

    @pl.when(step == 0)
    def _():
        square[...] = jnp.zeros_like(square)
        square[0:species, 0:species] = r_ref[...]
        square[species:padded, 0:species] = r_ref[0 : padded - species, :]
        high, low = split2(square[:, 0:padded])
        rs_ref[0:padded] = high
        rs_ref[padded : 2 * padded] = low

        tall[...] = jnp.zeros_like(tall)
        tall[:, 0:species] = k_ref[...]
        rows[...] = jnp.zeros_like(rows)
        factors = split3(a_ref[...] * LOG2E)
        energies = split3(e_ref[...] * LOG2E)
        order = [factors[0], factors[1], factors[2]] + [energies[i] for i in (0, 0, 0, 1, 1, 2)]
        for i, row in enumerate(order):
            rows[padded + i : padded + i + 1, 0:reactions] = row.astype(F32)
        for start in range(0, reactions, LANES):
            size = min(LANES, reactions - start)
            turned = rows[:, start : start + LANES].T[0:size]
            high, low = split2(tall[start : start + size, :])
            ka_ref[start : start + size, 0:LANES] = high + turned.astype(BF16)
            ka_ref[start : start + size, LANES : 2 * LANES] = low

        wide[...] = jnp.zeros_like(wide)
        wide[0:species] = m_ref[...]
        high, low = split2(wide[...])
        ms_ref[0:padded] = high
        ms_ref[padded : 2 * padded] = low
        peak_ref[...] = jnp.zeros_like(peak_ref)
        cols_ref[...] = jnp.zeros_like(cols_ref)

    flat = x_ref.reshape(species * CHUNK, LANES)
    lane = lane_index((padded, LANES))
    edges = jnp.zeros((padded, LANES), F32)
    peak = jnp.zeros((padded, LANES), F32)
    for pair in range(0, CHUNK, 2):
        for r in (pair, pair + 1):
            c_ref[r, 0:species] = flat[pl.ds(r, species, stride=CHUNK), :]
            c_ref[r, species:padded] = t_ref[r : r + 1, :]
        cells = jnp.concatenate([c_ref[pair], c_ref[pair + 1]], axis=1)
        spread = mixture(cells, rs_ref)
        d_ref[pair] = spread[:, 0:LANES]
        d_ref[pair + 1] = spread[:, LANES:]
        peak = jnp.maximum(peak, jnp.maximum(spread[:, 0:LANES], spread[:, LANES:]))
        for r in (pair, pair + 1):
            row = cells[:, (r - pair) * LANES : (r - pair + 1) * LANES]
            edges = jnp.where(lane == r, pltpu.roll(row, r, 1) if r else row, edges)
            edges = jnp.where(lane == 64 + r, pltpu.roll(row, 65 + r, 1), edges)
    moved = pltpu.roll(edges, step * CHUNK, 1)
    mine = jnp.bitwise_and(lane, 63) // CHUNK == step
    cols_ref[...] = jnp.where(mine, moved, cols_ref[...])

    @pl.when(step == 0)
    def _():
        top_ref[...] = c_ref[0]

    @pl.when(step == pl.num_programs(0) - 1)
    def _():
        bottom_ref[...] = c_ref[CHUNK - 1]

    best = jnp.maximum(peak_ref[...], jnp.max(jnp.max(peak, axis=0, keepdims=True), axis=1, keepdims=True))
    peak_ref[...] = best


def advance_kernel(
    species, reactions,
    flag_ref, peak_ref, c_ref, d_ref, up_ref, down_ref, left_ref, right_ref, cols_ref,
    t_ref, rs_ref, ka_ref, ms_ref, cool_ref,
    out_hbm, heat_ref,
    v_ref, edge_ref, outer_ref, gap_ref, order_ref, base_ref, k_ref, sum_ref, log_ref, high_ref, low_ref,
    cool_col, sems,
):
    row_count, padded, _ = c_ref.shape
    lane = lane_index((padded, LANES))

    def gather(x, found):
        order_ref[found] = x
        return found + flag_ref[x]

    live = lax.fori_loop(0, row_count, gather, jnp.int32(0))

    largest = jnp.max(peak_ref[...], axis=1, keepdims=True)
    half_step = 0.5 * (COURANT / largest)

    left = pltpu.roll(left_ref[...], 64, 1)
    right = pltpu.roll(right_ref[...], 64, 1)
    beyond = jnp.where(lane < 64, left, right)
    mine = cols_ref[...]
    spread = mixture(jnp.concatenate([mine, beyond], axis=1), rs_ref)
    edge_ref[...] = (spread[:, 0:LANES] + spread[:, LANES:]) * (beyond - mine)
    spread = mixture(jnp.concatenate([up_ref[...], down_ref[...]], axis=1), rs_ref)
    outer_ref[0] = spread[:, 0:LANES]
    outer_ref[1] = spread[:, LANES:]

    def row_flux(x, below, below_spread):
        here = c_ref[x]
        here_spread = d_ref[x]
        gap = (here_spread + below_spread) * (below - here)
        after = pltpu.roll(here, LANES - 1, 1)
        after_spread = pltpu.roll(here_spread, LANES - 1, 1)
        flux = (here_spread + after_spread) * (after - here)
        edge = edge_ref[...]
        flux = jnp.where(lane == LANES - 1, pltpu.roll(edge, 63 - x, 1), flux)
        before = jnp.where(lane == 0, -pltpu.roll(edge, LANES - x, 1), pltpu.roll(flux, 1, 1))
        v_ref[x] = here + half_step * ((flux - before) + (gap - gap_ref[...]))
        gap_ref[...] = gap

    gap_ref[...] = (d_ref[0] + outer_ref[0]) * (c_ref[0] - up_ref[...])

    @pl.loop(0, row_count - 1)
    def _(x):
        row_flux(x, c_ref[x + 1], d_ref[x + 1])
        pltpu.make_async_copy(v_ref.at[x, pl.ds(0, species)], out_hbm.at[:, x, :], sems.at[0]).start()

    row_flux(row_count - 1, down_ref[...], outer_ref[1])
    pltpu.make_async_copy(v_ref.at[row_count - 1, pl.ds(0, species)], out_hbm.at[:, row_count - 1, :], sems.at[0]).start()

    heat_ref[...] = t_ref[...]
    cool_col[...] = jnp.broadcast_to(cool_ref[...], cool_col.shape)

    def wait_rows(x, _):
        pltpu.make_async_copy(v_ref.at[0, pl.ds(0, species)], out_hbm.at[:, 0, :], sems.at[0]).wait()
        return 0

    lax.fori_loop(0, row_count, wait_rows, 0)

    log_ref[...] = jnp.zeros_like(log_ref)
    ceiling = RATE_CEILING * LOG2E

    def production(state):
        high, low = split2(jnp.log2(jnp.abs(state) + LOG_OFFSET))
        log_ref[0:padded] = high
        log_ref[LANES : LANES + padded] = high
        log_ref[2 * LANES : 2 * LANES + padded] = low
        log_ref[3 * LANES : 3 * LANES + padded] = low
        for start in range(0, reactions, 112):
            table = ka_ref[start : start + 112]
            rate = mxu(table, log_ref[0 : 2 * LANES]) + mxu(table, log_ref[2 * LANES : 4 * LANES])
            rate = jnp.exp2(jnp.minimum(rate, ceiling))
            high, low = split2(rate)
            high_ref[start : start + 112] = high
            low_ref[start : start + 112] = low
        both = mxu(ms_ref[...], high_ref[...])
        return both[0:padded] + both[padded:] + mxu(ms_ref[0:padded], low_ref[...])

    @pl.loop(0, (live + GROUP - 1) // GROUP)
    def _(group):
        places = [order_ref[jnp.minimum(group * GROUP + i, live - 1)] for i in range(GROUP)]
        for i, x in enumerate(places):
            base_ref[:, i * LANES : (i + 1) * LANES] = v_ref[x]
        heat = jnp.concatenate([t_ref[pl.ds(x, 1), :] for x in places], axis=1)
        parts = split3(-1.0 / heat)
        one = jnp.ones_like(parts[0])
        zero = jnp.zeros_like(one)
        extra = [one, one, one] + [parts[i] for i in (0, 1, 2, 0, 1, 0)] + [zero] * 7
        log_ref[padded:LANES] = jnp.concatenate(extra, axis=0)

        k_ref[...] = production(base_ref[...])
        sum_ref[...] = k_ref[...]
        k_ref[...] = production(base_ref[...] + 0.5 * CHEM_STEP * k_ref[...])
        sum_ref[...] += 2.0 * k_ref[...]
        k_ref[...] = production(base_ref[...] + 0.5 * CHEM_STEP * k_ref[...])
        sum_ref[...] += 2.0 * k_ref[...]
        total = sum_ref[...] + production(base_ref[...] + CHEM_STEP * k_ref[...])
        change = CHEM_STEP / 6.0 * total
        result = base_ref[...] + change
        moved = result - base_ref[...]
        for i, x in enumerate(places):
            lanes = slice(i * LANES, (i + 1) * LANES)
            drop = jnp.sum(cool_col[...] * moved[:, lanes], axis=0, keepdims=True)
            heat_ref[pl.ds(x, 1), :] = t_ref[pl.ds(x, 1), :] - drop

        for i, x in enumerate(places):
            @pl.when(group * GROUP + i < live)
            def _():
                v_ref[x] = result[:, i * LANES : (i + 1) * LANES]
                pltpu.make_async_copy(v_ref.at[x, pl.ds(0, species)], out_hbm.at[:, x, :], sems.at[1]).start()

    def wait_live(x, _):
        pltpu.make_async_copy(v_ref.at[0, pl.ds(0, species)], out_hbm.at[:, 0, :], sems.at[1]).wait()
        return 0

    lax.fori_loop(0, live, wait_live, 0)


def per_device(levels, heat, inverse, factor, exponents, energies, change, cooling, flags):
    row_count, species, _ = levels.shape
    reactions = factor.shape[0]
    padded = -(-species // 16) * 16
    across = -(-reactions // LANES) * LANES
    whole = pl.BlockSpec(memory_space=pltpu.VMEM)

    def fixed(*shape):
        return pl.BlockSpec(shape, lambda i: (0,) * len(shape))

    def shape(*dims, dtype=F32):
        return jax.ShapeDtypeStruct(dims, dtype)

    cells, spread, top, bottom, cols, peak, stacked, table, matrix = pl.pallas_call(
        functools.partial(spread_kernel, species, reactions),
        grid=(row_count // CHUNK,),
        in_specs=[
            pl.BlockSpec((species, CHUNK, LANES), lambda i: (0, i, 0)),
            pl.BlockSpec((CHUNK, LANES), lambda i: (i, 0)),
            fixed(species, species), fixed(1, reactions), fixed(reactions, species),
            fixed(1, reactions), fixed(species, reactions),
        ],
        out_specs=[
            pl.BlockSpec((CHUNK, padded, LANES), lambda i: (i, 0, 0)),
            pl.BlockSpec((CHUNK, padded, LANES), lambda i: (i, 0, 0)),
            fixed(padded, LANES), fixed(padded, LANES), fixed(padded, LANES), fixed(1, LANES),
            fixed(2 * padded, padded), fixed(reactions, 2 * LANES), fixed(2 * padded, reactions),
        ],
        out_shape=[
            shape(row_count, padded, LANES), shape(row_count, padded, LANES),
            shape(padded, LANES), shape(padded, LANES), shape(padded, LANES), shape(1, LANES),
            shape(2 * padded, padded, dtype=BF16), shape(reactions, 2 * LANES, dtype=BF16),
            shape(2 * padded, reactions, dtype=BF16),
        ],
        scratch_shapes=[
            pltpu.VMEM((padded, LANES), F32), pltpu.VMEM((LANES, across), F32),
            pltpu.VMEM((reactions, LANES), F32), pltpu.VMEM((padded, reactions), F32),
        ],
        compiler_params=pltpu.CompilerParams(vmem_limit_bytes=24 * 2**20),
        name="spread",
    )(
        levels.transpose(1, 0, 2), heat, inverse, factor.reshape(1, -1), exponents,
        energies.reshape(1, -1), change,
    )

    def neighbour(value, axis, ahead):
        count = lax.axis_size(axis)
        pairs = [(i, i + 1) if ahead else (i + 1, i) for i in range(count - 1)]
        return lax.ppermute(value, axis, pairs)

    up = neighbour(bottom, FLOW, True)
    down = neighbour(top, FLOW, False)
    left = neighbour(cols, "chem", True)
    right = neighbour(cols, "chem", False)
    peaks = lax.all_to_all(peak.reshape(-1), FLOW_CHEM, 0, 0, tiled=True).reshape(1, -1)

    wide = GROUP * LANES
    out, heat_out = pl.pallas_call(
        functools.partial(advance_kernel, species, reactions),
        in_specs=[pl.BlockSpec(memory_space=pltpu.SMEM)] + [whole] * 13,
        out_specs=[pl.BlockSpec(memory_space=pl.ANY), whole],
        out_shape=[shape(species, row_count, LANES), shape(row_count, LANES)],
        scratch_shapes=[
            pltpu.VMEM((row_count, padded, LANES), F32),
            pltpu.VMEM((padded, LANES), F32),
            pltpu.VMEM((2, padded, LANES), F32),
            pltpu.VMEM((padded, LANES), F32),
            pltpu.SMEM((row_count + 1,), jnp.int32),
            pltpu.VMEM((padded, wide), F32),
            pltpu.VMEM((padded, wide), F32),
            pltpu.VMEM((padded, wide), F32),
            pltpu.VMEM((4 * LANES, wide), BF16),
            pltpu.VMEM((reactions, wide), BF16),
            pltpu.VMEM((reactions, wide), BF16),
            pltpu.VMEM((padded, LANES), F32),
            pltpu.SemaphoreType.DMA((2,)),
        ],
        compiler_params=pltpu.CompilerParams(vmem_limit_bytes=40 * 2**20),
        name="advance",
    )(
        flags.reshape(-1), peaks, cells, spread, up, down, left, right, cols, heat,
        stacked, table, matrix, jnp.pad(cooling, (0, padded - species)).reshape(-1, 1),
    )
    return out.transpose(1, 0, 2), heat_out


def solution(mesh):
    torus = Mesh(
        mesh.devices.reshape(4, 4, 2, mesh.shape["chem"]), ("flow_0", "flow_1", "flow_2", "chem")
    )
    placed = (P(FLOW, None, "chem"), P(FLOW, "chem"), P(), P(), P(), P(), P(), P(), P(FLOW, "chem"))
    return jax.shard_map(
        per_device,
        mesh=torus,
        in_specs=placed,
        out_specs=(P(FLOW, None, "chem"), P(FLOW, "chem")),
        check_vma=False,
    )
```

profile of v0, /device:TPU:87, one launch (start us, length us, event | category | flops | bytes accessed | tf_op | source)
XLA Modules:
  0.0 89.8 jit_solution(8887392610739436493)
XLA Ops:
  0.6 0.0 copy-start.11
  0.6 0.0 copy-start.10
  0.7 0.7 reshape.25.a_ref
  1.4 0.7 reshape.26.e_ref
  2.0 0.0 copy-start.4
  2.0 2.0 %copy-done.4 = f32[64,111,128]{2,0,1:T(8,128)S(1)} copy-done((f32[64,111,128]{2,0,1:T(8,128)S(1)}, f32[64,111,128]{2,0,1:T(8,128)}, u32[]{:S(2)}) %copy-start.4) | copy-done | bytes 3637272
  4.1 0.0 copy-start.5
  4.1 1.0 %copy-done.5 = f32[784,111]{1,0:T(8,128)S(1)} copy-done((f32[784,111]{1,0:T(8,128)S(1)}, f32[784,111]{1,0:T(8,128)}, u32[]{:S(2)}) %copy-start.5) | copy-done | bytes 348120
  5.1 0.0 copy-start.6
  5.1 1.0 %copy-done.6 = f32[111,784]{1,0:T(8,128)S(1)} copy-done((f32[111,784]{1,0:T(8,128)S(1)}, f32[111,784]{1,0:T(8,128)}, u32[]{:S(2)}) %copy-start.6) | copy-done | bytes 348120
  6.1 0.0 copy-start.7
  6.1 0.8 copy-done.7
  6.8 0.0 copy-start.9
  6.8 0.8 copy-done.9
  7.6 0.0 copy-start.8
  7.7 5.1 %spread.1 = (f32[64,112,128]{2,1,0:T(8,128)S(1)}, f32[64,112,128]{2,1,0:T(8,128)S(1)}, f32[112,128]{1,0:T(8,128)S(1)}, f32[112,128]{1,0:T(8,128)S(1)}, f32[112,1...) custom-call(f32[111,64,128]{2,1,0:T(8,128)S(1)} %bitcast.7, ...), custom_call_target="tpu_custom_call" | custom-call | tf_op jit(solution)/shard_map/spread/pallas_call | solution.py:265
  12.7 0.0 copy-start
  12.7 1.8 %copy-done = f32[64,112,128]{2,1,0:T(8,128)} copy-done((f32[64,112,128]{2,1,0:T(8,128)}, f32[64,112,128]{2,1,0:T(8,128)S(1)}, u32[]{:S(2)}) %copy-start) | copy-done | bytes 3670040
  14.5 0.0 copy-start.2
  14.5 1.9 %copy-done.2 = f32[64,112,128]{2,1,0:T(8,128)} copy-done((f32[64,112,128]{2,1,0:T(8,128)}, f32[64,112,128]{2,1,0:T(8,128)S(1)}, u32[]{:S(2)}) %copy-start.2) | copy-done | bytes 3670040
  16.4 1.9 %collective-permute-start.3 = (f32[112,128]{1,0:T(8,128)S(1)}, f32[112,128]{1,0:T(8,128)S(1)}, u32[]{:S(2)}, u32[]{:S(2)}) collective-permute-start(f32[112,128]{1,0:T(8,128)S(1)} %get-tuple-element.18.cols_ref), channel_id=1, source_target_pairs={{1,0},{2,1},{3,2},{5,4},{6,5},{7,6},{9,8},{10,9},{11,10},{13,12},{... | collective-permute-start | bytes 172040 | tf_op jit(solution)/shard_map/ppermute | solution.py:300
  18.3 3.4 %collective-permute-start.2 = (f32[112,128]{1,0:T(8,128)S(1)}, f32[112,128]{1,0:T(8,128)S(1)}, u32[]{:S(2)}, u32[]{:S(2)}) collective-permute-start(f32[112,128]{1,0:T(8,128)S(1)} %get-tuple-element.18.cols_ref), channel_id=1, source_target_pairs={{0,1},{1,2},{2,3},{4,5},{5,6},{6,7},{8,9},{9,10},{10,11},{12,13},{... | collective-permute-start | bytes 172040 | tf_op jit(solution)/shard_map/ppermute | solution.py:300
  21.6 0.7 copy.14
  22.4 10.6 %all-to-all-start = ((f32[128,1,1]{2,1,0:T(1,128)}), f32[128,1,1]{2,1,0:T(1,128)S(1)}, u32[]{:S(2)}, u32[]{:S(2)}) async-start(f32[128,1,1]{2,1,0:T(1,128)} %copy.14), calls=%async_computation | async-start | bytes 131072 | tf_op jit(solution)/shard_map/all_to_all | solution.py:306
  33.0 3.1 %collective-permute-start = (f32[112,128]{1,0:T(8,128)S(1)}, f32[112,128]{1,0:T(8,128)S(1)}, u32[]{:S(2)}, u32[]{:S(2)}) collective-permute-start(f32[112,128]{1,0:T(8,128)S(1)} %get-tuple-element.16), channel_id=1, source_target_pairs={{0,4},{4,8},{8,12},{12,16},{16,20},{20,24},{24,28},{28,32},{32,36}... | collective-permute-start | bytes 172040 | tf_op jit(solution)/shard_map/ppermute | solution.py:300
  36.1 1.9 %collective-permute-start.1 = (f32[112,128]{1,0:T(8,128)S(1)}, f32[112,128]{1,0:T(8,128)S(1)}, u32[]{:S(2)}, u32[]{:S(2)}) collective-permute-start(f32[112,128]{1,0:T(8,128)S(1)} %get-tuple-element.17), channel_id=1, source_target_pairs={{4,0},{8,4},{12,8},{16,12},{20,16},{24,20},{28,24},{32,28},{36,32}... | collective-permute-start | bytes 172040 | tf_op jit(solution)/shard_map/ppermute | solution.py:300
  38.0 0.0 copy-done.11
  38.0 0.1 copy.15.cool_ref
  38.1 0.0 all-to-all-done
  38.1 1.0 %reduce = f32[128]{0:T(128)S(1)} reduce(f32[128,1,1]{2,1,0:T(1,128)S(1)} %all-to-all-done, f32[]{:T(128)} %constant.6), dimensions={1,2}, to_apply=%all_to_all.7.reduce_sub_computation | reduce | bytes 1028 | tf_op jit(solution)/shard_map/all_to_all | solution.py:306
  39.2 0.0 collective-permute-done.up_ref
  39.2 4.5 %collective-permute-done.1.down_ref = f32[112,128]{1,0:T(8,128)S(1)} collective-permute-done((f32[112,128]{1,0:T(8,128)S(1)}, f32[112,128]{1,0:T(8,128)S(1)}, u32[]{:S(2)}, u32[]{:S(2)}) %collective-permute-start.1) | collective-permute-done | bytes 57376 | tf_op jit(solution)/shard_map/ppermute | solution.py:300
  43.7 0.0 collective-permute-done.3.right_ref
  43.7 0.0 collective-permute-done.2.left_ref
  43.7 0.0 copy-done.10
  43.7 0.0 copy-done.8
  43.7 0.0 copy-start.1
  43.7 2.0 %copy-done.1 = f32[64,112,128]{2,1,0:T(8,128)S(1)} copy-done((f32[64,112,128]{2,1,0:T(8,128)S(1)}, f32[64,112,128]{2,1,0:T(8,128)}, u32[]{:S(2)}) %copy-start.1) | copy-done | bytes 3670040
  45.7 0.0 copy-start.3
  45.8 2.0 %copy-done.3 = f32[64,112,128]{2,1,0:T(8,128)S(1)} copy-done((f32[64,112,128]{2,1,0:T(8,128)S(1)}, f32[64,112,128]{2,1,0:T(8,128)}, u32[]{:S(2)}) %copy-start.3) | copy-done | bytes 3670040
  47.8 42.0 %advance.1 = (f32[111,64,128]{2,1,0:T(8,128)}, f32[64,128]{1,0:T(8,128)}) custom-call(s32[64]{0:T(128)S(1)} %bitcast.10, f32[1,128]{1,0:T(1,128)S(1)} %bitcast.8, f32[64,112,128]{2,1,0:T(8,128)S(1)} %copy-done.1, f32[64,112,128]{2,1,0:T(8,128)S(1)} %copy-done.3, f32[112,128]{1,0:T(8,128)S(1)} %collective-permute-done.up_ref, ...), custom_call_target="tpu_custom_call" | custom-call | tf_op jit(solution)/shard_map/advance/pallas_call | solution.py:309
  (1 shorter events, 0.0 us)
Async XLA Ops:
  0.6 37.4 %copy-start.11 = (f32[111]{0:T(128)S(1)}, f32[111]{0:T(128)}, u32[]{:S(2)}) copy-start(f32[111]{0:T(128)} %param.16) | copy-start | bytes 1336
  0.6 43.1 %copy-start.10 = (s32[64,1]{0,1:T(1,128)S(1)}, s32[64,1]{0,1:T(1,128)}, u32[]{:S(2)}) copy-start(s32[64,1]{0,1:T(1,128)} %param.17) | copy-start | bytes 772
  2.0 2.0 %copy-start.4 = (f32[64,111,128]{2,0,1:T(8,128)S(1)}, f32[64,111,128]{2,0,1:T(8,128)}, u32[]{:S(2)}) copy-start(f32[64,111,128]{2,0,1:T(8,128)} %param.9) | copy-start | bytes 10911748
  4.1 1.0 %copy-start.5 = (f32[784,111]{1,0:T(8,128)S(1)}, f32[784,111]{1,0:T(8,128)}, u32[]{:S(2)}) copy-start(f32[784,111]{1,0:T(8,128)} %k_ref.1) | copy-start | bytes 1044292
  5.1 1.0 %copy-start.6 = (f32[111,784]{1,0:T(8,128)S(1)}, f32[111,784]{1,0:T(8,128)}, u32[]{:S(2)}) copy-start(f32[111,784]{1,0:T(8,128)} %m_ref.1) | copy-start | bytes 1044292
  6.1 0.8 copy-start.7
  6.8 0.8 copy-start.9
  7.6 36.1 %copy-start.8 = (f32[64,128]{1,0:T(8,128)S(1)}, f32[64,128]{1,0:T(8,128)}, u32[]{:S(2)}) copy-start(f32[64,128]{1,0:T(8,128)} %t_ref.3) | copy-start | bytes 98308
  12.7 1.8 %copy-start = (f32[64,112,128]{2,1,0:T(8,128)}, f32[64,112,128]{2,1,0:T(8,128)S(1)}, u32[]{:S(2)}) copy-start(f32[64,112,128]{2,1,0:T(8,128)S(1)} %get-tuple-element.14.c_ref) | copy-start | bytes 11010052
  14.5 1.9 %copy-start.2 = (f32[64,112,128]{2,1,0:T(8,128)}, f32[64,112,128]{2,1,0:T(8,128)S(1)}, u32[]{:S(2)}) copy-start(f32[64,112,128]{2,1,0:T(8,128)S(1)} %get-tuple-element.15.d_ref) | copy-start | bytes 11010052
  16.4 27.3 %collective-permute-start.3 = (f32[112,128]{1,0:T(8,128)S(1)}, f32[112,128]{1,0:T(8,128)S(1)}, u32[]{:S(2)}, u32[]{:S(2)}) collective-permute-start(f32[112,128]{1,0:T(8,128)S(1)} %get-tuple-element.18.cols_ref), channel_id=1, source_target_pairs={{1,0},{2,1},{3,2},{5,4},{6,5},{7,6},{9,8},{10,9},{11,10},{13,12},{... | collective-permute-start | bytes 172040 | tf_op jit(solution)/shard_map/ppermute | solution.py:300
  18.3 25.4 %collective-permute-start.2 = (f32[112,128]{1,0:T(8,128)S(1)}, f32[112,128]{1,0:T(8,128)S(1)}, u32[]{:S(2)}, u32[]{:S(2)}) collective-permute-start(f32[112,128]{1,0:T(8,128)S(1)} %get-tuple-element.18.cols_ref), channel_id=1, source_target_pairs={{0,1},{1,2},{2,3},{4,5},{5,6},{6,7},{8,9},{9,10},{10,11},{12,13},{... | collective-permute-start | bytes 172040 | tf_op jit(solution)/shard_map/ppermute | solution.py:300
  22.4 15.8 %all-to-all-start = ((f32[128,1,1]{2,1,0:T(1,128)}), f32[128,1,1]{2,1,0:T(1,128)S(1)}, u32[]{:S(2)}, u32[]{:S(2)}) async-start(f32[128,1,1]{2,1,0:T(1,128)} %copy.14), calls=%async_computation | async-start | bytes 131072 | tf_op jit(solution)/shard_map/all_to_all | solution.py:306
  33.0 6.2 %collective-permute-start = (f32[112,128]{1,0:T(8,128)S(1)}, f32[112,128]{1,0:T(8,128)S(1)}, u32[]{:S(2)}, u32[]{:S(2)}) collective-permute-start(f32[112,128]{1,0:T(8,128)S(1)} %get-tuple-element.16), channel_id=1, source_target_pairs={{0,4},{4,8},{8,12},{12,16},{16,20},{20,24},{24,28},{28,32},{32,36}... | collective-permute-start | bytes 172040 | tf_op jit(solution)/shard_map/ppermute | solution.py:300
  36.1 7.6 %collective-permute-start.1 = (f32[112,128]{1,0:T(8,128)S(1)}, f32[112,128]{1,0:T(8,128)S(1)}, u32[]{:S(2)}, u32[]{:S(2)}) collective-permute-start(f32[112,128]{1,0:T(8,128)S(1)} %get-tuple-element.17), channel_id=1, source_target_pairs={{4,0},{8,4},{12,8},{16,12},{20,16},{24,20},{28,24},{32,28},{36,32}... | collective-permute-start | bytes 172040 | tf_op jit(solution)/shard_map/ppermute | solution.py:300
  43.7 2.0 %copy-start.1 = (f32[64,112,128]{2,1,0:T(8,128)S(1)}, f32[64,112,128]{2,1,0:T(8,128)}, u32[]{:S(2)}) copy-start(f32[64,112,128]{2,1,0:T(8,128)} %copy-done) | copy-start | bytes 11010052
  45.7 2.0 %copy-start.3 = (f32[64,112,128]{2,1,0:T(8,128)S(1)}, f32[64,112,128]{2,1,0:T(8,128)}, u32[]{:S(2)}) copy-start(f32[64,112,128]{2,1,0:T(8,128)} %copy-done.2) | copy-start | bytes 11010052
where the time goes:
time: 90.7 us; the launch traced here: 89.8 us
  Pallas kernels  47.1 us (52%)
  starting transfers between devices  20.9 us (23%)
  local copies, waits for them, and re-layouts  15.6 us (17%)
  waiting for transfers between devices  4.52 us (5%)
  other arithmetic  1.03 us (1%)
    pallas_call x1, Pallas kernels, per_device(): pl.pallas_call(functools.partial(advance_kernel, species, reactions), in_...  42 us
    unnamed x24, local copies, waits for them, and re-layouts  13.3 us
    all_to_all x1, starting transfers between devices, per_device(): lax.all_to_all(peak.reshape(-1), FLOW_CHEM, 0, 0, tiled=True).reshape(1, -1)  10.6 us
    ppermute x4, starting transfers between devices, neighbour(): return lax.ppermute(value, axis, pairs)  10.3 us
    pallas_call x1, Pallas kernels, per_device(): pl.pallas_call(functools.partial(spread_kernel, species, reactions), grid...  5.06 us
    ppermute x4, waiting for transfers between devices, neighbour(): return lax.ppermute(value, axis, pairs)  4.52 us
  transfers between devices with their start and end apart: 5, of which 1 were waited for; matrix products, arithmetic and copies ran while one was open for 2% of the time, Pallas kernels for 0%

commit v1 on v0

v1 whole, which is shorter than its diff:
```python
import functools

import jax
import jax.numpy as jnp
from jax import lax
from jax.experimental import pallas as pl
from jax.experimental.pallas import tpu as pltpu
from jax.sharding import Mesh
from jax.sharding import PartitionSpec as P

FLOW = ("flow_0", "flow_1", "flow_2")
FLOW_CHEM = ("flow_0", "flow_1", "flow_2", "chem")

COURANT = 0.2
CHEM_STEP = 0.05
LOG_OFFSET = 0.001
RATE_CEILING = 2.0
LOG2E = 1.4426950408889634

F32 = jnp.float32
BF16 = jnp.bfloat16
LANES = 128
GROUP = 4
CHUNK = 8
HALF = 4


def split2(value):
    high = value.astype(BF16)
    return high, (value - high.astype(F32)).astype(BF16)


def split3(value):
    high = value.astype(BF16)
    rest = value - high.astype(F32)
    mid = rest.astype(BF16)
    return high, mid, (rest - mid.astype(F32)).astype(BF16)


def mxu(lhs, rhs):
    return jnp.dot(lhs, rhs, preferred_element_type=F32)


def mixture(cells, stacked):
    padded = cells.shape[0]
    high, low = split2(cells)
    both = mxu(stacked[...], high)
    total = both[:padded] + both[padded:] + mxu(stacked[0:padded], low)
    heat = cells[padded - 1 : padded]
    there = heat > 0.0
    scaled = heat * jnp.sqrt(heat)
    return jnp.where(there, scaled, 0.0) / jnp.where(there, total, 1.0)


def lane_index(shape):
    return lax.broadcasted_iota(jnp.int32, shape, len(shape) - 1)


def spread_kernel(
    species, reactions,
    x_hbm, t_hbm, r_hbm, a_ref, k_hbm, e_ref, m_hbm, cool_ref,
    c_hbm, d_hbm, even_ref, odd_ref, cols_ref, peak_ref, rs_ref, ka_ref, ms_ref, mr_ref, cool_col,
    x_buf, c_buf, d_buf, heat, square, rows, tall, wide, first_col, last_col, in_sems, small_sems, out_sem,
):
    row_count, padded, _ = c_buf.shape
    chunks = row_count // CHUNK
    full = ms_ref.shape[1]

    def chunk_in(i):
        return pltpu.make_async_copy(x_hbm.at[:, pl.ds(i * CHUNK, CHUNK)], x_buf.at[i], in_sems.at[i])

    heat_in = pltpu.make_async_copy(t_hbm, heat, small_sems.at[0])
    heat_in.start()
    chunk_in(0).start()
    inverse_in = pltpu.make_async_copy(r_hbm, square, small_sems.at[1])
    inverse_in.start()
    for i in range(1, chunks):
        chunk_in(i).start()
    exponents_in = pltpu.make_async_copy(k_hbm, tall, small_sems.at[2])
    exponents_in.start()
    change_in = pltpu.make_async_copy(m_hbm, wide, small_sems.at[3])
    change_in.start()

    rows[...] = jnp.zeros_like(rows)
    factors = split3(a_ref[...].reshape(1, reactions) * LOG2E)
    energies = split3(e_ref[...].reshape(1, reactions) * LOG2E)
    order = [factors[0], factors[1], factors[2]] + [energies[i] for i in (0, 0, 0, 1, 1, 2)]
    for i, row in enumerate(order):
        rows[padded + i : padded + i + 1, 0:reactions] = row.astype(F32)
    rows[0:1, reactions : reactions + species] = cool_ref[...].reshape(1, species)

    inverse_in.wait()
    high, low = split2(square[...])
    none = jnp.zeros((species, padded - species), BF16)
    for first, part in ((0, high), (padded, low)):
        part = jnp.concatenate([part, none], axis=1)
        rs_ref[first : first + padded] = jnp.concatenate([part, part[0 : padded - species]], axis=0)

    heat_in.wait()
    lane = lane_index((padded, LANES))
    def chunk(i, peak):
        chunk_in(i).wait()
        flat = x_buf.at[i].reshape(species * CHUNK, LANES)
        base = i * CHUNK
        first = jnp.zeros((padded, LANES), F32)
        last = jnp.zeros((padded, LANES), F32)
        for pair in range(0, CHUNK, 2):
            for r in (pair, pair + 1):
                c_buf[base + r, 0:species] = flat[pl.ds(r, species, stride=CHUNK), :]
                c_buf[base + r, species:padded] = heat[pl.ds(base + r, 1), :]
            cells = jnp.concatenate([c_buf[base + pair], c_buf[base + pair + 1]], axis=1)
            spread = mixture(cells, rs_ref)
            d_buf[base + pair] = spread[:, 0:LANES]
            d_buf[base + pair + 1] = spread[:, LANES:]
            peak = jnp.maximum(peak, jnp.maximum(spread[:, 0:LANES], spread[:, LANES:]))
            for r in (pair, pair + 1):
                row = cells[:, (r - pair) * LANES : (r - pair + 1) * LANES]
                row = pltpu.roll(row, r, 1) if r else row
                first = jnp.where(lane == r, row, first)
                last = jnp.where(lane == (r - 1) % LANES, row, last)
        here = lane // CHUNK == i
        first_col[...] = jnp.where(here, pltpu.roll(first, base, 1), first_col[...])
        last_col[...] = jnp.where(here, pltpu.roll(last, base + 1, 1), last_col[...])
        rows_here = pl.ds(base, CHUNK)
        pltpu.make_async_copy(c_buf.at[rows_here], c_hbm.at[rows_here], out_sem).start()
        pltpu.make_async_copy(d_buf.at[rows_here], d_hbm.at[rows_here], out_sem).start()
        return peak

    first_col[...] = jnp.zeros_like(first_col)
    last_col[...] = jnp.zeros_like(last_col)
    peak = lax.fori_loop(0, chunks, chunk, jnp.zeros((padded, LANES), F32))
    best = jnp.max(jnp.max(peak, axis=0, keepdims=True), axis=1, keepdims=True)
    peak_ref[...] = jnp.broadcast_to(best, peak_ref.shape)
    cols_ref[...] = jnp.where(lane < 64, first_col[...], pltpu.roll(last_col[...], 64, 1))
    flipped = lax.axis_index(FLOW[-1]) * (row_count - 1)
    even_ref[...] = c_buf[row_count - 1 - flipped]
    odd_ref[...] = c_buf[flipped]

    exponents_in.wait()
    for start in range(0, reactions, LANES):
        size = min(LANES, reactions - start)
        turned = rows[:, start : start + LANES].T[0:size]
        high, low = split2(tall[start : start + size, :])
        none = jnp.zeros((size, LANES - species), BF16)
        spare = lane_index((size, LANES)) >= padded
        high = jnp.concatenate([high, none], axis=1)
        ka_ref[start : start + size, 0:LANES] = jnp.where(spare, turned.astype(BF16), high)
        ka_ref[start : start + size, LANES : 2 * LANES] = jnp.concatenate([low, none], axis=1)
    cool_col[...] = jnp.broadcast_to(rows[:, reactions : reactions + LANES].T[0:padded, 0:1], cool_col.shape)
    change_in.wait()
    high, low = split2(wide[...])
    none = jnp.zeros((padded - species, reactions), BF16)
    high = jnp.concatenate([high, none], axis=0)
    low = jnp.concatenate([low, none], axis=0)
    ms_ref[0:padded] = high[:, 0:full]
    ms_ref[padded : 2 * padded] = low[:, 0:full]
    mr_ref[...] = jnp.concatenate([high[:, full:], low[:, full:], high[:, full:]], axis=1)

    pltpu.make_async_copy(c_buf, c_hbm, out_sem).wait()
    pltpu.make_async_copy(d_buf, d_hbm, out_sem).wait()


def flux_kernel(
    c_hbm, d_hbm, even_ref, odd_ref, pair_ref, cross_ref, cols_ref, rs_ref, s_hbm,
    c_ref, d_ref, s_ref, first_ref, last_ref, gap_ref, step_ref, in_sems, out_sem,
):
    row_count, padded, _ = s_ref.shape
    chunks = row_count // CHUNK
    lane = lane_index((padded, LANES))

    def chunk_in(i):
        here = pl.ds(i * CHUNK, CHUNK)
        return (
            pltpu.make_async_copy(c_hbm.at[here], c_ref.at[here], in_sems.at[0, i]),
            pltpu.make_async_copy(d_hbm.at[here], d_ref.at[here], in_sems.at[1, i]),
        )

    for i in range(chunks):
        for copy in chunk_in(i):
            copy.start()

    odd = lax.axis_index(FLOW[-1]) == 1
    above = jnp.where(odd, even_ref[...], odd_ref[...])
    below = jnp.where(odd, odd_ref[...], even_ref[...])
    odd = lax.rem(lax.axis_index("chem"), 2) == 1
    left = jnp.where(odd, pair_ref[...], cross_ref[...])
    right = jnp.where(odd, cross_ref[...], pair_ref[...])
    beyond = pltpu.roll(jnp.where(lane < 64, right, left), 64, 1)
    mine = cols_ref[...]
    spread = mixture(jnp.concatenate([mine, beyond], axis=1), rs_ref)
    edge = (spread[:, 0:LANES] + spread[:, LANES:]) * (beyond - mine)
    first_ref[...] = edge
    last_ref[...] = pltpu.roll(edge, 63, 1)
    outer = mixture(jnp.concatenate([above, below], axis=1), rs_ref)
    c_ref[row_count] = below
    d_ref[row_count] = outer[:, LANES:]

    rows = jnp.bitwise_and(lax.broadcasted_iota(jnp.int32, (2 * LANES, 2 * LANES), 0), LANES - 1)
    cell = lane_index((2 * LANES, 2 * LANES))
    back = cell >= LANES
    cell = jnp.bitwise_and(cell, LANES - 1)
    beside = jnp.where(back, cell - 1, cell + 1)
    inside = jnp.logical_and(beside >= 0, beside < LANES)
    there = jnp.where(jnp.logical_and(inside, rows == beside), 1.0, 0.0)
    here = jnp.where(jnp.logical_and(inside, rows == cell), 1.0, 0.0)
    step_ref[0] = (there - here).astype(BF16)
    step_ref[1] = (there + here).astype(BF16)

    def wait_in(i):
        for copy in chunk_in(i):
            copy.wait()

    def beside_of(ref, base, which):
        value = ref[pl.ds(base, HALF)].reshape(HALF * padded, LANES)
        return mxu(jnp.concatenate(split2(value), axis=1), step_ref[which])

    wait_in(0)
    gap_ref[...] = (d_ref[0] + outer[:, 0:LANES]) * (c_ref[0] - above)

    @pl.loop(0, row_count // HALF)
    def _(part):
        base = part * HALF

        @pl.when(jnp.logical_and(part % 2 == 1, part < row_count // HALF - 1))
        def _():
            wait_in(part // 2 + 1)

        change = beside_of(c_ref, base, 0)
        total = beside_of(d_ref, base, 1)
        along = change * total
        along = along[:, 0:LANES] + along[:, LANES:]
        gap = gap_ref[...]
        for r in range(HALF):
            x = base + r
            later = (d_ref[x] + d_ref[x + 1]) * (c_ref[x + 1] - c_ref[x])
            ends = pltpu.roll(jnp.where(lane == x, first_ref[...], last_ref[...]), LANES - x, 1)
            ends = jnp.where(jnp.logical_or(lane == 0, lane == LANES - 1), ends, 0.0)
            s_ref[x] = (along[r * padded : (r + 1) * padded] + ends) + (later - gap)
            gap = later
        gap_ref[...] = gap

        @pl.when(part % 2 == 1)
        def _():
            done = pl.ds((part // 2) * CHUNK, CHUNK)
            pltpu.make_async_copy(s_ref.at[done], s_hbm.at[done], out_sem).start()

    pltpu.make_async_copy(s_ref, s_hbm, out_sem).wait()


def advance_kernel(
    species, reactions,
    flag_ref, peak_ref, c_hbm, s_hbm, ka_ref, ms_ref, mr_ref, cool_col,
    out_hbm, heat_ref,
    c_ref, s_ref, o_ref, order_ref, base_ref, k_ref, sum_ref, log_ref, high_ref, low_ref, rest_ref,
    in_sems, out_sem,
):
    row_count, padded, _ = c_ref.shape
    full = high_ref.shape[0]
    chunks = row_count // CHUNK

    def chunk_in(i):
        here = pl.ds(i * CHUNK, CHUNK)
        return (
            pltpu.make_async_copy(c_hbm.at[here], c_ref.at[here], in_sems.at[0, i]),
            pltpu.make_async_copy(s_hbm.at[here], s_ref.at[here], in_sems.at[1, i]),
        )

    for i in range(chunks):
        for copy in chunk_in(i):
            copy.start()

    def gather(x, found):
        order_ref[found] = x
        return found + flag_ref[x]

    live = lax.fori_loop(0, row_count, gather, jnp.int32(0))
    order_ref[live] = row_count

    largest = jnp.max(jnp.max(peak_ref[...], axis=0, keepdims=True), axis=1, keepdims=True)
    half_step = jnp.broadcast_to(0.5 * (COURANT / largest), (padded, LANES))
    flat_out = o_ref.reshape(row_count * species, LANES)

    def put(x, value):
        first = (x // CHUNK) * (CHUNK * species) + jnp.bitwise_and(x, CHUNK - 1)
        flat_out[pl.ds(first, species, stride=CHUNK), :] = value[0:species]

    @pl.loop(0, chunks)
    def _(i):
        for copy in chunk_in(i):
            copy.wait()
        for r in range(CHUNK):
            x = i * CHUNK + r
            value = c_ref[x] + half_step * s_ref[x]
            c_ref[x, 0:species] = value[0:species]
            flat_out[pl.ds(i * (CHUNK * species) + r, species, stride=CHUNK), :] = value[0:species]
            heat_ref[pl.ds(x, 1), :] = c_ref[x, padded - 1 : padded]

    def send(i, _):
        pltpu.make_async_copy(o_ref.at[i], out_hbm.at[:, pl.ds(i * CHUNK, CHUNK)], out_sem).start()
        return 0

    sent = order_ref[0] // CHUNK
    lax.fori_loop(0, sent, send, 0)

    log_ref[...] = jnp.zeros_like(log_ref)
    ceiling = RATE_CEILING * LOG2E

    def production(state):
        high, low = split2(jnp.log2(jnp.abs(state) + LOG_OFFSET))
        log_ref[0:padded] = high
        log_ref[LANES : LANES + padded] = high
        log_ref[2 * LANES : 2 * LANES + padded] = low
        log_ref[3 * LANES : 3 * LANES + padded] = low
        for start in range(0, reactions, LANES):
            size = min(LANES, reactions - start)
            table = ka_ref[start : start + size]
            rate = mxu(table, log_ref[0 : 2 * LANES]) + mxu(table, log_ref[2 * LANES : 4 * LANES])
            high, low = split2(jnp.exp2(jnp.minimum(rate, ceiling)))
            if start < full:
                high_ref[start : start + size] = high
                low_ref[start : start + size] = low
            else:
                rest_ref[...] = jnp.concatenate([high, high, low], axis=0)
        both = mxu(ms_ref[...], high_ref[...])
        return (both[0:padded] + both[padded:]) + mxu(ms_ref[0:padded], low_ref[...]) + mxu(mr_ref[...], rest_ref[...])

    @pl.loop(0, (live + GROUP - 1) // GROUP, init_carry=sent)
    def sent(group, sent):
        places = [order_ref[jnp.minimum(group * GROUP + i, live - 1)] for i in range(GROUP)]
        for i, x in enumerate(places):
            base_ref[:, i * LANES : (i + 1) * LANES] = c_ref[x]
        heat = base_ref[padded - 1 : padded]
        parts = split3(-1.0 / heat)
        one = jnp.ones_like(parts[0])
        zero = jnp.zeros_like(one)
        extra = [one, one, one] + [parts[i] for i in (0, 1, 2, 0, 1, 0)] + [zero] * 7
        log_ref[padded:LANES] = jnp.concatenate(extra, axis=0)

        k_ref[...] = production(base_ref[...])
        sum_ref[...] = k_ref[...]
        k_ref[...] = production(base_ref[...] + 0.5 * CHEM_STEP * k_ref[...])
        sum_ref[...] += 2.0 * k_ref[...]
        k_ref[...] = production(base_ref[...] + 0.5 * CHEM_STEP * k_ref[...])
        sum_ref[...] += 2.0 * k_ref[...]
        total = sum_ref[...] + production(base_ref[...] + CHEM_STEP * k_ref[...])
        result = base_ref[...] + CHEM_STEP / 6.0 * total
        moved = result - base_ref[...]
        for i, x in enumerate(places):
            lanes = slice(i * LANES, (i + 1) * LANES)
            put(x, result[:, lanes])
            drop = jnp.sum(cool_col[...] * moved[:, lanes], axis=0, keepdims=True)
            heat_ref[pl.ds(x, 1), :] = base_ref[padded - 1 : padded, lanes] - drop

        done = order_ref[jnp.minimum(group * GROUP + GROUP, live)] // CHUNK
        lax.fori_loop(sent, done, send, 0)
        return done

    lax.fori_loop(sent, chunks, send, 0)

    def wait_out(i, _):
        pltpu.make_async_copy(o_ref.at[0], out_hbm.at[:, pl.ds(0, CHUNK)], out_sem).wait()
        return 0

    lax.fori_loop(0, chunks, wait_out, 0)


def per_device(levels, heat, inverse, factor, exponents, energies, change, cooling, flags):
    row_count, species, _ = levels.shape
    reactions = factor.shape[0]
    padded = -(-species // 16) * 16
    across = -(-reactions // LANES) * LANES + LANES
    chunks = row_count // CHUNK
    full = reactions // LANES * LANES
    rest = reactions - full
    devices = 1
    for axis in FLOW_CHEM:
        devices *= lax.axis_size(axis)
    near = pl.BlockSpec(memory_space=pltpu.VMEM)
    far = pl.BlockSpec(memory_space=pltpu.HBM)

    def shape(*dims, dtype=F32):
        return jax.ShapeDtypeStruct(dims, dtype)

    plane = (row_count, padded, LANES)
    cells, spread, even, odd, cols, peak, stacked, table, matrix, narrow, cool_col = pl.pallas_call(
        functools.partial(spread_kernel, species, reactions),
        in_specs=[far, far, far, near, far, near, far, near],
        out_specs=[far, far] + [near] * 9,
        out_shape=[
            shape(*plane), shape(*plane),
            shape(padded, LANES), shape(padded, LANES), shape(padded, LANES), shape(devices, LANES),
            shape(2 * padded, padded, dtype=BF16), shape(reactions, 2 * LANES, dtype=BF16),
            shape(2 * padded, full, dtype=BF16), shape(padded, 3 * rest, dtype=BF16), shape(padded, LANES),
        ],
        scratch_shapes=[
            pltpu.VMEM((chunks, species, CHUNK, LANES), F32), pltpu.VMEM(plane, F32), pltpu.VMEM(plane, F32),
            pltpu.VMEM((row_count, LANES), F32), pltpu.VMEM((species, species), F32),
            pltpu.VMEM((LANES, across), F32), pltpu.VMEM((reactions, species), F32),
            pltpu.VMEM((species, reactions), F32),
            pltpu.VMEM((padded, LANES), F32), pltpu.VMEM((padded, LANES), F32),
            pltpu.SemaphoreType.DMA((chunks,)), pltpu.SemaphoreType.DMA((4,)), pltpu.SemaphoreType.DMA,
        ],
        cost_estimate=pl.CostEstimate(flops=10**9, bytes_accessed=11 * 10**6, transcendentals=0),
        name="spread",
    )(levels.transpose(1, 0, 2), heat, inverse, factor, exponents, energies, change, cooling)

    def swap(value, axis, first):
        pairs = []
        for i in range(first, lax.axis_size(axis) - 1, 2):
            pairs += [(i, i + 1), (i + 1, i)]
        return lax.ppermute(value, axis, pairs)

    peaks = lax.all_to_all(peak, FLOW_CHEM, 0, 0, tiled=True)
    even = swap(even, FLOW, 0)
    odd = swap(odd, FLOW, 1)
    pair = swap(cols, "chem", 0)
    cross = swap(cols, "chem", 1)

    fluxes = pl.pallas_call(
        flux_kernel,
        in_specs=[far, far] + [near] * 6,
        out_specs=far,
        out_shape=shape(*plane),
        scratch_shapes=[
            pltpu.VMEM((row_count + 1, padded, LANES), F32), pltpu.VMEM((row_count + 1, padded, LANES), F32),
            pltpu.VMEM(plane, F32), pltpu.VMEM((padded, LANES), F32), pltpu.VMEM((padded, LANES), F32),
            pltpu.VMEM((padded, LANES), F32), pltpu.VMEM((2, 2 * LANES, 2 * LANES), BF16),
            pltpu.SemaphoreType.DMA((2, chunks)), pltpu.SemaphoreType.DMA,
        ],
        cost_estimate=pl.CostEstimate(flops=10**9, bytes_accessed=11 * 10**6, transcendentals=0),
        name="flux",
    )(cells, spread, even, odd, pair, cross, cols, stacked)

    span = GROUP * LANES
    out, heat_out = pl.pallas_call(
        functools.partial(advance_kernel, species, reactions),
        in_specs=[pl.BlockSpec(memory_space=pltpu.SMEM), near, far, far, near, near, near, near],
        out_specs=[far, near],
        out_shape=[shape(species, row_count, LANES), shape(row_count, LANES)],
        scratch_shapes=[
            pltpu.VMEM(plane, F32), pltpu.VMEM(plane, F32), pltpu.VMEM((chunks, species, CHUNK, LANES), F32),
            pltpu.SMEM((row_count + 1,), jnp.int32),
            pltpu.VMEM((padded, span), F32), pltpu.VMEM((padded, span), F32), pltpu.VMEM((padded, span), F32),
            pltpu.VMEM((4 * LANES, span), BF16),
            pltpu.VMEM((full, span), BF16), pltpu.VMEM((full, span), BF16), pltpu.VMEM((3 * rest, span), BF16),
            pltpu.SemaphoreType.DMA((2, chunks)), pltpu.SemaphoreType.DMA,
        ],
        cost_estimate=pl.CostEstimate(flops=2 * 10**10, bytes_accessed=11 * 10**6, transcendentals=0),
        name="advance",
    )(flags.reshape(-1), peaks, cells, fluxes, table, matrix, narrow, cool_col)
    return out.transpose(1, 0, 2), heat_out


def solution(mesh):
    torus = Mesh(
        mesh.devices.reshape(4, 4, 2, mesh.shape["chem"]), ("flow_0", "flow_1", "flow_2", "chem")
    )
    placed = (P(FLOW, None, "chem"), P(FLOW, "chem"), P(), P(), P(), P(), P(), P(), P(FLOW, "chem"))
    return jax.shard_map(
        per_device,
        mesh=torus,
        in_specs=placed,
        out_specs=(P(FLOW, None, "chem"), P(FLOW, "chem")),
        check_vma=False,
    )
```

time: 90.7 us -> 65.8 us (0.73)
  local copies, waits for them, and re-layouts: 15.6 us -> 1.25 us
  starting transfers between devices: 20.9 us -> 15.4 us
  waiting for transfers between devices: 4.52 us -> 0.01 us
  other arithmetic: 1.03 us -> 0 us
    unnamed x24 -> x10, local copies, waits for them, and re-layouts: 13.3 us -> 1.25 us
    pallas_call x1 -> x2, Pallas kernels: 5.06 us -> 15.9 us  [the longest x1 8.17 us: per_device(): pl.pallas_call(flux_kernel, in_specs=[far, far] + [near] * 6, out_specs=f...]
    pallas_call x1, Pallas kernels: 42 us -> 31.9 us  [per_device(): pl.pallas_call(functools.partial(advance_kernel, species, reactions), in_...]
    ppermute x4, starting transfers between devices: 10.3 us -> 5.57 us  [swap(): return lax.ppermute(value, axis, pairs)]
    ppermute x4, waiting for transfers between devices: 4.52 us -> 0.01 us  [swap(): return lax.ppermute(value, axis, pairs)]
    reshape x4 -> x0, local copies, waits for them, and re-layouts: 1.5 us -> none  [the longest x1 0.7 us: per_device(): factor.reshape(1, -1)]
    all_to_all x1 -> x0, other arithmetic: 1.03 us -> none  [per_device(): lax.all_to_all(peak.reshape(-1), FLOW_CHEM, 0, 0, tiled=True).reshape(1, -1)]
  transfers between devices with their start and end apart: 5 -> 5, of which waited for: 1 -> 0; matrix products, arithmetic and copies ran while one was open for 2% -> 0% of each run, Pallas kernels for 0% -> 13%
where the time goes in v1:
time: 65.8 us; the launch traced here: 65.1 us
  Pallas kernels  47.8 us (73%)
  starting transfers between devices  15.4 us (23%)
  local copies, waits for them, and re-layouts  1.25 us (2%)
  between operations  0.75 us (1%)
    pallas_call x1, Pallas kernels, per_device(): pl.pallas_call(functools.partial(advance_kernel, species, reactions), in_...  31.9 us
    all_to_all x1, starting transfers between devices, per_device(): peaks = lax.all_to_all(peak, FLOW_CHEM, 0, 0, tiled=True)  9.78 us
    pallas_call x1, Pallas kernels, per_device(): pl.pallas_call(flux_kernel, in_specs=[far, far] + [near] * 6, out_specs=f...  8.17 us
    pallas_call x1, Pallas kernels, per_device(): pl.pallas_call(functools.partial(spread_kernel, species, reactions), in_s...  7.72 us
    ppermute x4, starting transfers between devices, swap(): return lax.ppermute(value, axis, pairs)  5.57 us
  transfers between devices with their start and end apart: 5, of which 0 were waited for; matrix products, arithmetic and copies ran while one was open for 0% of the time, Pallas kernels for 13%

profile of v1, /device:TPU:87, one launch (start us, length us, event | category | flops | bytes accessed | tf_op | source)
XLA Modules:
  0.0 65.1 jit_solution(2273265011056771462)
XLA Ops:
  0.6 7.7 %spread.1 = (f32[64,112,128]{2,1,0:T(8,128)}, f32[64,112,128]{2,1,0:T(8,128)}, f32[112,128]{1,0:T(8,128)}, f32[112,128]{1,0:T(8,128)}, f32[112,128]{1,0:T(8,128)...) custom-call(f32[111,64,128]{2,1,0:T(8,128)} %bitcast.7, ...), custom_call_target="tpu_custom_call" | custom-call | flops 1000000000 | bytes 11000000 | tf_op jit(solution)/shard_map/spread/pallas_call | solution.py:385
  8.4 0.8 %collective-permute-start = (f32[112,128]{1,0:T(8,128)}, f32[112,128]{1,0:T(8,128)S(1)}, u32[]{:S(2)}, u32[]{:S(2)}) collective-permute-start(f32[112,128]{1,0:T(8,128)} %get-tuple-element.18), channel_id=1, source_target_pairs={{0,4},{4,0},{8,12},{12,8},{16,20},{20,16},{24,28},{28,24},{32,36},... | collective-permute-start | bytes 172040 | tf_op jit(solution)/shard_map/ppermute | solution.py:411
  9.1 2.7 %collective-permute-start.1 = (f32[112,128]{1,0:T(8,128)}, f32[112,128]{1,0:T(8,128)S(1)}, u32[]{:S(2)}, u32[]{:S(2)}) collective-permute-start(f32[112,128]{1,0:T(8,128)} %get-tuple-element.19), channel_id=1, source_target_pairs={{4,8},{8,4},{12,16},{16,12},{20,24},{24,20},{28,32},{32,28},{36,40... | collective-permute-start | bytes 172040 | tf_op jit(solution)/shard_map/ppermute | solution.py:411
  11.9 1.9 %collective-permute-start.3 = (f32[112,128]{1,0:T(8,128)}, f32[112,128]{1,0:T(8,128)S(1)}, u32[]{:S(2)}, u32[]{:S(2)}) collective-permute-start(f32[112,128]{1,0:T(8,128)} %get-tuple-element.20.cols_ref), channel_id=1, source_target_pairs={{1,2},{2,1},{5,6},{6,5},{9,10},{10,9},{13,14},{14,13},{17,18},{18,... | collective-permute-start | bytes 172040 | tf_op jit(solution)/shard_map/ppermute | solution.py:411
  13.8 0.2 collective-permute-start.2
  13.9 9.8 %all-to-all-start = ((f32[128,1,128]{2,1,0:T(1,128)}), f32[128,1,128]{2,1,0:T(1,128)S(1)}, u32[]{:S(2)}, u32[]{:S(2)}) async-start(f32[128,1,128]{2,1,0:T(1,128)} %bitcast.8), calls=%async_computation | async-start | bytes 131072 | tf_op jit(solution)/shard_map/all_to_all | solution.py:413
  23.7 0.0 collective-permute-done.even_ref
  23.7 0.0 copy-start.1
  23.8 0.0 collective-permute-done.1.odd_ref
  23.8 0.0 copy-start.2
  23.8 0.0 collective-permute-done.3.cross_ref
  23.8 0.0 copy-start.3
  23.8 0.0 collective-permute-done.2.pair_ref
  23.8 0.0 copy-start.4
  23.8 0.6 copy-done.1
  24.4 0.0 copy-done.2
  24.4 0.0 copy-done.3
  24.4 0.0 copy-done.4
  24.4 8.2 %flux.1.s_hbm = f32[64,112,128]{2,1,0:T(8,128)} custom-call(f32[64,112,128]{2,1,0:T(8,128)} %get-tuple-element.16.c_hbm, f32[64,112,128]{2,1,0:T(8,128)} %get-tuple-element.17.d_hbm, f32[112,128]{1,0:T(8,128)} %copy-done.1, f32[112,128]{1,0:T(8,128)} %copy-done.2, f32[112,128]{1,0:T(8,128)} %copy-done.4, f32[112,128]{1,0:T(8,128)} %copy-done.3, ...), custom_call_target="tpu_custom_call" | custom-call | flops 1000000000 | bytes 11000000 | tf_op jit(solution)/shard_map/flux/pallas_call | solution.py:419
  32.6 0.0 all-to-all-done
  32.6 0.0 copy-start
  32.6 0.6 copy-done
  33.3 31.9 %advance.1 = (f32[111,64,128]{2,1,0:T(8,128)}, f32[64,128]{1,0:T(8,128)}) custom-call(s32[64]{0:T(128)} %bitcast.10, f32[128,128]{1,0:T(8,128)} %bitcast.9, f32[64,112,128]{2,1,0:T(8,128)} %get-tuple-element.16.c_hbm, f32[64,112,128]{2,1,0:T(8,128)} %flux.1.s_hbm, bf16[784,256]{1,0:T(8,128)(2,1)} %get-tuple-element.22.ka_ref, ...), custom_call_target="tpu_custom_call" | custom-call | flops 20000000000 | bytes 11000000 | tf_op jit(solution)/shard_map/advance/pallas_call | solution.py:435
Async XLA Ops:
  8.4 15.4 %collective-permute-start = (f32[112,128]{1,0:T(8,128)}, f32[112,128]{1,0:T(8,128)S(1)}, u32[]{:S(2)}, u32[]{:S(2)}) collective-permute-start(f32[112,128]{1,0:T(8,128)} %get-tuple-element.18), channel_id=1, source_target_pairs={{0,4},{4,0},{8,12},{12,8},{16,20},{20,16},{24,28},{28,24},{32,36},... | collective-permute-start | bytes 172040 | tf_op jit(solution)/shard_map/ppermute | solution.py:411
  9.1 14.6 %collective-permute-start.1 = (f32[112,128]{1,0:T(8,128)}, f32[112,128]{1,0:T(8,128)S(1)}, u32[]{:S(2)}, u32[]{:S(2)}) collective-permute-start(f32[112,128]{1,0:T(8,128)} %get-tuple-element.19), channel_id=1, source_target_pairs={{4,8},{8,4},{12,16},{16,12},{20,24},{24,20},{28,32},{32,28},{36,40... | collective-permute-start | bytes 172040 | tf_op jit(solution)/shard_map/ppermute | solution.py:411
  11.9 11.9 %collective-permute-start.3 = (f32[112,128]{1,0:T(8,128)}, f32[112,128]{1,0:T(8,128)S(1)}, u32[]{:S(2)}, u32[]{:S(2)}) collective-permute-start(f32[112,128]{1,0:T(8,128)} %get-tuple-element.20.cols_ref), channel_id=1, source_target_pairs={{1,2},{2,1},{5,6},{6,5},{9,10},{10,9},{13,14},{14,13},{17,18},{18,... | collective-permute-start | bytes 172040 | tf_op jit(solution)/shard_map/ppermute | solution.py:411
  13.8 10.0 %collective-permute-start.2 = (f32[112,128]{1,0:T(8,128)}, f32[112,128]{1,0:T(8,128)S(1)}, u32[]{:S(2)}, u32[]{:S(2)}) collective-permute-start(f32[112,128]{1,0:T(8,128)} %get-tuple-element.20.cols_ref), channel_id=1, source_target_pairs={{0,1},{1,0},{2,3},{3,2},{4,5},{5,4},{6,7},{7,6},{8,9},{9,8},{10,11... | collective-permute-start | bytes 172040 | tf_op jit(solution)/shard_map/ppermute | solution.py:411
  13.9 18.7 %all-to-all-start = ((f32[128,1,128]{2,1,0:T(1,128)}), f32[128,1,128]{2,1,0:T(1,128)S(1)}, u32[]{:S(2)}, u32[]{:S(2)}) async-start(f32[128,1,128]{2,1,0:T(1,128)} %bitcast.8), calls=%async_computation | async-start | bytes 131072 | tf_op jit(solution)/shard_map/all_to_all | solution.py:413
  23.7 0.6 copy-start.1
  23.8 0.6 copy-start.2
  23.8 0.6 copy-start.3
  23.8 0.6 copy-start.4
  32.6 0.6 copy-start

commit v2 on v1

v2 whole, which is shorter than its diff:
```python
import functools

import jax
import jax.numpy as jnp
from jax import lax
from jax.experimental import pallas as pl
from jax.experimental.pallas import tpu as pltpu
from jax.sharding import Mesh
from jax.sharding import PartitionSpec as P

FLOW = ("flow_0", "flow_1", "flow_2")
FLOW_CHEM = ("flow_0", "flow_1", "flow_2", "chem")

COURANT = 0.2
CHEM_STEP = 0.05
LOG_OFFSET = 0.001
RATE_CEILING = 2.0
LOG2E = 1.4426950408889634

F32 = jnp.float32
BF16 = jnp.bfloat16
LANES = 128
GROUP = 4
STREAMS = 2
SPAN = 784
CHUNK = 8
HALF = 4


def split2(value):
    high = value.astype(BF16)
    return high, (value - high.astype(F32)).astype(BF16)


def split3(value):
    high = value.astype(BF16)
    rest = value - high.astype(F32)
    mid = rest.astype(BF16)
    return high, mid, (rest - mid.astype(F32)).astype(BF16)


def mxu(lhs, rhs):
    return jnp.dot(lhs, rhs, preferred_element_type=F32)


def mixture(cells, stacked):
    padded = cells.shape[0]
    high, low = split2(cells)
    both = mxu(stacked[...], high)
    total = both[:padded] + both[padded:] + mxu(stacked[0:padded], low)
    heat = cells[padded - 1 : padded]
    there = heat > 0.0
    scaled = heat * jnp.sqrt(heat)
    return jnp.where(there, scaled, 0.0) / jnp.where(there, total, 1.0)


def lane_index(shape):
    return lax.broadcasted_iota(jnp.int32, shape, len(shape) - 1)


def stack_inverse(stacked, inverse):
    species = inverse.shape[0]
    padded = stacked.shape[0] // 2
    none = jnp.zeros((species, padded - species), BF16)
    for first, part in zip((0, padded), split2(inverse[...])):
        part = jnp.concatenate([part, none], axis=1)
        stacked[first : first + padded] = jnp.concatenate([part, part[0 : padded - species]], axis=0)


def spread_kernel(
    species,
    x_hbm, t_hbm, r_hbm,
    c_hbm, d_hbm, even_hbm, odd_hbm, cols_hbm, peak_hbm,
    cols_ref, peak_ref, x_buf, c_buf, d_buf, heat, square, rs_ref, first_col, last_col, in_sems, small_sems, end_sems, out_sem,
):
    row_count, padded, _ = c_buf.shape
    chunks = row_count // CHUNK

    def chunk_in(i):
        return pltpu.make_async_copy(x_hbm.at[:, pl.ds(i * CHUNK, CHUNK)], x_buf.at[i], in_sems.at[i])

    chunk_in(0).start()
    heat_in = pltpu.make_async_copy(t_hbm, heat, small_sems.at[0])
    heat_in.start()
    inverse_in = pltpu.make_async_copy(r_hbm, square, small_sems.at[1])
    inverse_in.start()
    for i in range(1, chunks):
        chunk_in(i).start()

    first_col[...] = jnp.zeros_like(first_col)
    last_col[...] = jnp.zeros_like(last_col)
    lane = lane_index((padded, LANES))
    inverse_in.wait()
    stack_inverse(rs_ref, square)
    heat_in.wait()

    def send(buf, hbm, i):
        here = pl.ds(i * CHUNK, CHUNK)
        pltpu.make_async_copy(buf.at[here], hbm.at[here], out_sem).start()

    def chunk(i, peak):
        chunk_in(i).wait()
        flat = x_buf.at[i].reshape(species * CHUNK, LANES)
        base = i * CHUNK
        first = jnp.zeros((padded, LANES), F32)
        last = jnp.zeros((padded, LANES), F32)
        for pair in range(0, CHUNK, 2):
            x = base + pair
            for r in (pair, pair + 1):
                c_buf[base + r, 0:species] = flat[pl.ds(r, species, stride=CHUNK), :]
                c_buf[base + r, species:padded] = heat[pl.ds(base + r, 1), :]
            row = [c_buf[x], c_buf[x + 1]]
            high, low = split2(jnp.concatenate(row, axis=1))
            both = mxu(rs_ref[...], high)
            total = both[:padded] + both[padded:] + mxu(rs_ref[0:padded], low)
            warm = jnp.concatenate([heat[pl.ds(x, 1), :], heat[pl.ds(x + 1, 1), :]], axis=1)
            spread = warm * jnp.sqrt(warm) / total
            thin = [spread[:, 0:LANES], spread[:, LANES:]]
            peak = jnp.maximum(peak, jnp.maximum(thin[0], thin[1]))

            d_buf[x] = thin[0]
            d_buf[x + 1] = thin[1]
            for r, value in zip((pair, pair + 1), row):
                value = pltpu.roll(value, r, 1) if r else value
                first = jnp.where(lane == r, value, first)
                last = jnp.where(lane == (r - 1) % LANES, value, last)
        here = lane // CHUNK == i
        first_col[...] = jnp.where(here, pltpu.roll(first, base, 1), first_col[...])
        last_col[...] = jnp.where(here, pltpu.roll(last, base + 1, 1), last_col[...])
        send(c_buf, c_hbm, i)
        send(d_buf, d_hbm, i)
        return peak

    peak = lax.fori_loop(0, chunks, chunk, jnp.zeros((padded, LANES), F32))
    best = jnp.max(jnp.max(peak, axis=0, keepdims=True), axis=1, keepdims=True)
    peak_ref[...] = jnp.broadcast_to(best, peak_ref.shape)
    cols_ref[...] = jnp.where(lane < 64, first_col[...], pltpu.roll(last_col[...], 64, 1))
    flipped = lax.axis_index(FLOW[-1]) * (row_count - 1)
    ends = [
        pltpu.make_async_copy(src, dst, end_sems.at[n])
        for n, (src, dst) in enumerate((
            (peak_ref, peak_hbm), (cols_ref, cols_hbm),
            (c_buf.at[row_count - 1 - flipped], even_hbm), (c_buf.at[flipped], odd_hbm),
        ))
    ]
    for copy in ends:
        copy.start()
    for copy in ends:
        copy.wait()
    pltpu.make_async_copy(c_buf, c_hbm, out_sem).wait()
    pltpu.make_async_copy(d_buf, d_hbm, out_sem).wait()


def flux_kernel(
    c_hbm, d_hbm, even_hbm, odd_hbm, pair_hbm, cross_hbm, cols_hbm, r_hbm, s_hbm,
    c_ref, d_ref, s_ref, sides, square, rs_ref, first_ref, last_ref, gap_ref, step_ref, in_sems, small_sems, out_sem,
):
    row_count, padded, _ = s_ref.shape
    chunks = row_count // CHUNK
    lane = lane_index((padded, LANES))

    def chunk_in(i):
        here = pl.ds(i * CHUNK, CHUNK)
        return (
            pltpu.make_async_copy(c_hbm.at[here], c_ref.at[here], in_sems.at[0, i]),
            pltpu.make_async_copy(d_hbm.at[here], d_ref.at[here], in_sems.at[1, i]),
        )

    small = [pltpu.make_async_copy(r_hbm, square, small_sems.at[0])]
    for n, side in enumerate((even_hbm, odd_hbm, pair_hbm, cross_hbm, cols_hbm)):
        small.append(pltpu.make_async_copy(side, sides.at[n], small_sems.at[n + 1]))
    for copy in small:
        copy.start()
    for i in range(chunks):
        for copy in chunk_in(i):
            copy.start()

    rows = jnp.bitwise_and(lax.broadcasted_iota(jnp.int32, (2 * LANES, 2 * LANES), 0), LANES - 1)
    cell = lane_index((2 * LANES, 2 * LANES))
    back = cell >= LANES
    cell = jnp.bitwise_and(cell, LANES - 1)
    beside = jnp.where(back, cell - 1, cell + 1)
    inside = jnp.logical_and(beside >= 0, beside < LANES)
    there = jnp.where(jnp.logical_and(inside, rows == beside), 1.0, 0.0)
    here = jnp.where(jnp.logical_and(inside, rows == cell), 1.0, 0.0)
    step_ref[0] = (there - here).astype(BF16)
    step_ref[1] = (there + here).astype(BF16)
    for copy in small:
        copy.wait()
    stack_inverse(rs_ref, square)

    odd = lax.axis_index(FLOW[-1]) == 1
    above = jnp.where(odd, sides[0], sides[1])
    below = jnp.where(odd, sides[1], sides[0])
    odd = lax.rem(lax.axis_index("chem"), 2) == 1
    left = jnp.where(odd, sides[2], sides[3])
    right = jnp.where(odd, sides[3], sides[2])
    beyond = pltpu.roll(jnp.where(lane < 64, right, left), 64, 1)
    mine = sides[4]
    spread = mixture(jnp.concatenate([mine, beyond], axis=1), rs_ref)
    edge = (spread[:, 0:LANES] + spread[:, LANES:]) * (beyond - mine)
    first_ref[...] = edge
    last_ref[...] = pltpu.roll(edge, 63, 1)
    outer = mixture(jnp.concatenate([above, below], axis=1), rs_ref)
    c_ref[row_count] = below
    d_ref[row_count] = outer[:, LANES:]

    def wait_in(i):
        for copy in chunk_in(i):
            copy.wait()

    def beside_of(ref, base, which):
        value = ref[pl.ds(base, HALF)].reshape(HALF * padded, LANES)
        return mxu(jnp.concatenate(split2(value), axis=1), step_ref[which])

    wait_in(0)
    gap_ref[...] = (d_ref[0] + outer[:, 0:LANES]) * (c_ref[0] - above)

    @pl.loop(0, row_count // HALF)
    def _(part):
        base = part * HALF

        @pl.when(jnp.logical_and(part % 2 == 1, part < row_count // HALF - 1))
        def _():
            wait_in(part // 2 + 1)

        change = beside_of(c_ref, base, 0)
        total = beside_of(d_ref, base, 1)
        along = change * total
        along = along[:, 0:LANES] + along[:, LANES:]
        gap = gap_ref[...]
        for r in range(HALF):
            x = base + r
            later = (d_ref[x] + d_ref[x + 1]) * (c_ref[x + 1] - c_ref[x])
            ends = pltpu.roll(jnp.where(lane == x, first_ref[...], last_ref[...]), LANES - x, 1)
            ends = jnp.where(jnp.logical_or(lane == 0, lane == LANES - 1), ends, 0.0)
            s_ref[x] = (along[r * padded : (r + 1) * padded] + ends) + (later - gap)
            gap = later
        gap_ref[...] = gap

        @pl.when(part % 2 == 1)
        def _():
            done = pl.ds((part // 2) * CHUNK, CHUNK)
            pltpu.make_async_copy(s_ref.at[done], s_hbm.at[done], out_sem).start()

    pltpu.make_async_copy(s_ref, s_hbm, out_sem).wait()


def advance_kernel(
    species, reactions,
    flag_hbm, peak_hbm, c_hbm, s_hbm, a_hbm, k_hbm, e_hbm, m_hbm, cool_hbm,
    out_hbm, heat_hbm,
    flag_ref, a_ref, e_ref, cool_ref, heat_ref, c_ref, s_ref, o_ref, order_ref, half_ref, peaks, rows, tall, wide,
    ka_ref, ms_ref, mr_ref, cool_col, small_sems, early_sems, heat_sem, *rest,
):
    streams = [rest[i * 7 : i * 7 + 7] for i in range(STREAMS)]
    in_sems, out_sem = rest[STREAMS * 7 :]
    row_count, padded, _ = c_ref.shape
    full = ms_ref.shape[1]
    chunks = row_count // CHUNK
    together = STREAMS * GROUP

    def chunk_in(i):
        here = pl.ds(i * CHUNK, CHUNK)
        return (
            pltpu.make_async_copy(c_hbm.at[here], c_ref.at[here], in_sems.at[0, i]),
            pltpu.make_async_copy(s_hbm.at[here], s_ref.at[here], in_sems.at[1, i]),
        )

    small = [
        pltpu.make_async_copy(*ends, small_sems.at[n])
        for n, ends in enumerate(
            ((peak_hbm, peaks), (k_hbm, tall), (m_hbm, wide))
        )
    ]
    early = [
        pltpu.make_async_copy(*ends, early_sems.at[n])
        for n, ends in enumerate(((flag_hbm, flag_ref), (a_hbm, a_ref), (e_hbm, e_ref), (cool_hbm, cool_ref)))
    ]
    for copy in early:
        copy.start()
    for copy in small:
        copy.start()
    for i in range(chunks):
        for copy in chunk_in(i):
            copy.start()

    rows[...] = jnp.zeros_like(rows)
    for stream in streams:
        stream[3][...] = jnp.zeros_like(stream[3])
    for copy in early:
        copy.wait()
    factors = split3(a_ref[...].reshape(1, reactions) * LOG2E)
    energies = split3(e_ref[...].reshape(1, reactions) * LOG2E)
    order = [factors[0], factors[1], factors[2]] + [energies[i] for i in (0, 0, 0, 1, 1, 2)]
    for i, row in enumerate(order):
        rows[padded + i : padded + i + 1, 0:reactions] = row.astype(F32)
    rows[0:1, reactions : reactions + species] = cool_ref[...].reshape(1, species)
    cool_col[...] = jnp.broadcast_to(rows[:, reactions : reactions + LANES].T[0:padded, 0:1], cool_col.shape)

    def gather(x, found):
        order_ref[found] = x
        return found + flag_ref[x]

    live = lax.fori_loop(0, row_count, gather, jnp.int32(0))
    order_ref[live] = row_count

    for copy in small:
        copy.wait()
    for start in range(0, reactions, LANES):
        size = min(LANES, reactions - start)
        turned = rows[:, start : start + LANES].T[0:size]
        high, low = split2(tall[start : start + size, :])
        none = jnp.zeros((size, LANES - species), BF16)
        spare = lane_index((size, LANES)) >= padded
        high = jnp.concatenate([high, none], axis=1)
        ka_ref[start : start + size, 0:LANES] = jnp.where(spare, turned.astype(BF16), high)
        ka_ref[start : start + size, LANES : 2 * LANES] = jnp.concatenate([low, none], axis=1)
    none = jnp.zeros((padded - species, reactions), BF16)
    high, low = [jnp.concatenate([part, none], axis=0) for part in split2(wide[...])]
    ms_ref[0:padded] = high[:, 0:full]
    ms_ref[padded : 2 * padded] = low[:, 0:full]
    mr_ref[...] = jnp.concatenate([high[:, full:], low[:, full:], high[:, full:]], axis=1)
    largest = jnp.max(jnp.max(peaks[...], axis=0, keepdims=True), axis=1, keepdims=True)
    half_ref[...] = jnp.broadcast_to(0.5 * (COURANT / largest), half_ref.shape)
    flat_out = o_ref.reshape(row_count * species, LANES)

    def put(x, value):
        first = (x // CHUNK) * (CHUNK * species) + jnp.bitwise_and(x, CHUNK - 1)
        flat_out[pl.ds(first, species, stride=CHUNK), :] = value[0:species]

    def send(i, _):
        pltpu.make_async_copy(o_ref.at[i], out_hbm.at[:, pl.ds(i * CHUNK, CHUNK)], out_sem).start()
        return 0

    def quiet_rows(i, _):
        for copy in chunk_in(i):
            copy.wait()
        for r in range(CHUNK):
            x = i * CHUNK + r
            value = c_ref[x] + half_ref[...] * s_ref[x]
            c_ref[x, 0:species] = value[0:species]
            flat_out[pl.ds(i * (CHUNK * species) + r, species, stride=CHUNK), :] = value[0:species]
            heat_ref[pl.ds(x, 1), :] = c_ref[x, padded - 1 : padded]
        return 0

    lax.fori_loop(0, chunks, quiet_rows, 0)

    ceiling = RATE_CEILING * LOG2E

    def production(state, log_ref, high_ref, low_ref, rest_ref):
        high, low = split2(jnp.log2(jnp.abs(state) + LOG_OFFSET))
        log_ref[0:padded] = high
        log_ref[LANES : LANES + padded] = high
        log_ref[2 * LANES : 2 * LANES + padded] = low
        log_ref[3 * LANES : 3 * LANES + padded] = low
        for start in range(0, reactions, SPAN):
            stop = min(start + SPAN, reactions)
            table = ka_ref[start:stop]
            rate = mxu(table, log_ref[0 : 2 * LANES]) + mxu(table, log_ref[2 * LANES : 4 * LANES])
            high, low = split2(jnp.exp2(jnp.minimum(rate, ceiling)))
            inner = min(stop, full)
            high_ref[start:inner] = high[0 : inner - start]
            low_ref[start:inner] = low[0 : inner - start]
            if stop == reactions:
                rest_ref[...] = jnp.concatenate([high[full - start :], high[full - start :], low[full - start :]], axis=0)
        both = mxu(ms_ref[...], high_ref[...])
        return (both[0:padded] + both[padded:]) + mxu(ms_ref[0:padded], low_ref[...]) + mxu(mr_ref[...], rest_ref[...])

    def begin(places, base_ref, k_ref, sum_ref, log_ref, *_):
        for i, x in enumerate(places):
            base_ref[:, i * LANES : (i + 1) * LANES] = c_ref[x]
        heat = base_ref[padded - 1 : padded]
        parts = split3(-1.0 / heat)
        one = jnp.ones_like(parts[0])
        zero = jnp.zeros_like(one)
        extra = [one, one, one] + [parts[i] for i in (0, 1, 2, 0, 1, 0)] + [zero] * 7
        log_ref[padded:LANES] = jnp.concatenate(extra, axis=0)

    def section(index, base_ref, k_ref, sum_ref, *rest):
        if index == 0:
            k_ref[...] = production(base_ref[...], *rest)
            sum_ref[...] = k_ref[...]
        elif index < 3:
            k_ref[...] = production(base_ref[...] + 0.5 * CHEM_STEP * k_ref[...], *rest)
            sum_ref[...] += 2.0 * k_ref[...]
        else:
            sum_ref[...] += production(base_ref[...] + CHEM_STEP * k_ref[...], *rest)

    def finish(places, base_ref, k_ref, sum_ref, *_):
        result = base_ref[...] + CHEM_STEP / 6.0 * sum_ref[...]
        moved = result - base_ref[...]
        for i, x in enumerate(places):
            lanes = slice(i * LANES, (i + 1) * LANES)
            put(x, result[:, lanes])
            drop = jnp.sum(cool_col[...] * moved[:, lanes], axis=0, keepdims=True)
            heat_ref[pl.ds(x, 1), :] = base_ref[padded - 1 : padded, lanes] - drop

    def reach(count):
        return jnp.minimum(order_ref[jnp.minimum(count, live)] // CHUNK, chunks)

    sent = order_ref[0] // CHUNK
    lax.fori_loop(0, sent, send, 0)

    @pl.loop(0, (live + together - 1) // together, init_carry=sent)
    def sent(group, sent):
        first = group * together
        places = [
            [order_ref[jnp.minimum(first + n * GROUP + i, live - 1)] for i in range(GROUP)] for n in range(STREAMS)
        ]
        for rows, stream in zip(places, streams):
            begin(rows, *stream)
        for index in range(4):
            for stream in streams:
                section(index, *stream)
        for rows, stream in zip(places, streams):
            finish(rows, *stream)
        done = order_ref[jnp.minimum(first + together, live)] // CHUNK
        lax.fori_loop(sent, done, send, 0)
        return done

    lax.fori_loop(sent, chunks, send, 0)

    heat_out = pltpu.make_async_copy(heat_ref, heat_hbm, heat_sem)
    heat_out.start()

    def wait_out(i, _):
        pltpu.make_async_copy(o_ref.at[0], out_hbm.at[:, pl.ds(0, CHUNK)], out_sem).wait()
        return 0

    lax.fori_loop(0, chunks, wait_out, 0)
    heat_out.wait()


def per_device(levels, heat, inverse, factor, exponents, energies, change, cooling, flags):
    row_count, species, _ = levels.shape
    reactions = factor.shape[0]
    padded = -(-species // 16) * 16
    across = -(-reactions // LANES) * LANES + LANES
    chunks = row_count // CHUNK
    full = reactions // LANES * LANES
    rest = reactions - full
    devices = 1
    for axis in FLOW_CHEM:
        devices *= lax.axis_size(axis)
    far = pl.BlockSpec(memory_space=pltpu.HBM)

    def shape(*dims, dtype=F32):
        return jax.ShapeDtypeStruct(dims, dtype)

    plane = (row_count, padded, LANES)
    def side():
        return pltpu.VMEM((padded, LANES), F32)

    cells, spread, mine_even, mine_odd, cols, peak = pl.pallas_call(
        functools.partial(spread_kernel, species),
        in_specs=[far, far, far],
        out_specs=[far] * 6,
        out_shape=[
            shape(*plane), shape(*plane),
            shape(padded, LANES), shape(padded, LANES), shape(padded, LANES), shape(devices, LANES),
        ],
        scratch_shapes=[
            side(), pltpu.VMEM((devices, LANES), F32),
            pltpu.VMEM((chunks, species, CHUNK, LANES), F32), pltpu.VMEM(plane, F32), pltpu.VMEM(plane, F32),
            pltpu.VMEM((row_count, LANES), F32), pltpu.VMEM((species, species), F32),
            pltpu.VMEM((2 * padded, padded), BF16), side(), side(),
            pltpu.SemaphoreType.DMA((chunks,)), pltpu.SemaphoreType.DMA((2,)), pltpu.SemaphoreType.DMA((4,)),
            pltpu.SemaphoreType.DMA,
        ],
        cost_estimate=pl.CostEstimate(flops=10**9, bytes_accessed=11 * 10**6, transcendentals=0),
        name="spread",
    )(levels.transpose(1, 0, 2), heat, inverse)

    def swap(value, axis, first):
        pairs = []
        for i in range(first, lax.axis_size(axis) - 1, 2):
            pairs += [(i, i + 1), (i + 1, i)]
        return lax.ppermute(value, axis, pairs)

    peaks = lax.all_to_all(peak, FLOW_CHEM, 0, 0, tiled=True)
    even = swap(mine_even, FLOW, 0)
    odd = swap(mine_odd, FLOW, 1)
    pair = swap(cols, "chem", 0)
    cross = swap(cols, "chem", 1)

    fluxes = pl.pallas_call(
        flux_kernel,
        in_specs=[far] * 8,
        out_specs=far,
        out_shape=shape(*plane),
        scratch_shapes=[
            pltpu.VMEM((row_count + 1, padded, LANES), F32), pltpu.VMEM((row_count + 1, padded, LANES), F32),
            pltpu.VMEM(plane, F32), pltpu.VMEM((5, padded, LANES), F32), pltpu.VMEM((species, species), F32),
            pltpu.VMEM((2 * padded, padded), BF16), side(), side(), side(),
            pltpu.VMEM((2, 2 * LANES, 2 * LANES), BF16),
            pltpu.SemaphoreType.DMA((2, chunks)), pltpu.SemaphoreType.DMA((6,)), pltpu.SemaphoreType.DMA,
        ],
        cost_estimate=pl.CostEstimate(flops=10**9, bytes_accessed=11 * 10**6, transcendentals=0),
        name="flux",
    )(cells, spread, even, odd, pair, cross, cols, inverse)

    span = GROUP * LANES
    out, heat_out = pl.pallas_call(
        functools.partial(advance_kernel, species, reactions),
        in_specs=[far] * 9,
        out_specs=[far, far],
        out_shape=[shape(species, row_count, LANES), shape(row_count, LANES)],
        scratch_shapes=[
            pltpu.SMEM((row_count,), jnp.int32), pltpu.VMEM((reactions,), F32), pltpu.VMEM((reactions,), F32),
            pltpu.VMEM((species,), F32), pltpu.VMEM((row_count, LANES), F32),
            pltpu.VMEM(plane, F32), pltpu.VMEM(plane, F32), pltpu.VMEM((chunks, species, CHUNK, LANES), F32),
            pltpu.SMEM((row_count + 1,), jnp.int32), side(),
            pltpu.VMEM((devices, LANES), F32),
            pltpu.VMEM((LANES, across), F32), pltpu.VMEM((reactions, species), F32),
            pltpu.VMEM((species, reactions), F32), pltpu.VMEM((reactions, 2 * LANES), BF16),
            pltpu.VMEM((2 * padded, full), BF16), pltpu.VMEM((padded, 3 * rest), BF16),
            side(), pltpu.SemaphoreType.DMA((3,)),
            pltpu.SemaphoreType.DMA((4,)), pltpu.SemaphoreType.DMA,
        ]
        + STREAMS * [
            pltpu.VMEM((padded, span), F32), pltpu.VMEM((padded, span), F32), pltpu.VMEM((padded, span), F32),
            pltpu.VMEM((4 * LANES, span), BF16),
            pltpu.VMEM((full, span), BF16), pltpu.VMEM((full, span), BF16), pltpu.VMEM((3 * rest, span), BF16),
        ]
        + [
            pltpu.SemaphoreType.DMA((2, chunks)), pltpu.SemaphoreType.DMA,
        ],
        cost_estimate=pl.CostEstimate(flops=2 * 10**10, bytes_accessed=11 * 10**6, transcendentals=0),
        name="advance",
    )(
        flags.reshape(-1), peaks, cells, fluxes, factor, exponents, energies, change, cooling,
    )
    return out.transpose(1, 0, 2), heat_out


def solution(mesh):
    torus = Mesh(
        mesh.devices.reshape(4, 4, 2, mesh.shape["chem"]), ("flow_0", "flow_1", "flow_2", "chem")
    )
    placed = (P(FLOW, None, "chem"), P(FLOW, "chem"), P(), P(), P(), P(), P(), P(), P(FLOW, "chem"))
    return jax.shard_map(
        per_device,
        mesh=torus,
        in_specs=placed,
        out_specs=(P(FLOW, None, "chem"), P(FLOW, "chem")),
        check_vma=False,
    )
```

time: 65.8 us -> 59 us (0.90)
  the two profiles are of different devices: /device:TPU:87 before, /device:TPU:85 now
where the time goes in v2:
time: 59 us; the launch traced here: 58.3 us
  Pallas kernels  41 us (69%)
  starting transfers between devices  15.4 us (26%)
  local copies, waits for them, and re-layouts  1.23 us (2%)
  between operations  0.75 us (1%)
    pallas_call x1, Pallas kernels, per_device(): pl.pallas_call(functools.partial(advance_kernel, species, reactions), in_...  25.4 us
    all_to_all x1, starting transfers between devices, per_device(): peaks = lax.all_to_all(peak, FLOW_CHEM, 0, 0, tiled=True)  9.8 us
    pallas_call x1, Pallas kernels, per_device(): pl.pallas_call(flux_kernel, in_specs=[far] * 8, out_specs=far, out_shape=...  9.5 us
    pallas_call x1, Pallas kernels, per_device(): pl.pallas_call(functools.partial(spread_kernel, species), in_specs=[far,...  6.03 us
    ppermute x4, starting transfers between devices, swap(): return lax.ppermute(value, axis, pairs)  5.56 us
    unnamed x10, local copies, waits for them, and re-layouts  1.23 us
  transfers between devices with their start and end apart: 5, of which 0 were waited for; matrix products, arithmetic and copies ran while one was open for 0% of the time, Pallas kernels for 16%

profile of v2, /device:TPU:85, one launch (start us, length us, event | category | flops | bytes accessed | tf_op | source)
XLA Modules:
  0.0 58.3 jit_solution(8912993780512507709)
XLA Ops:
  0.6 6.0 %spread.1 = (f32[64,112,128]{2,1,0:T(8,128)}, f32[64,112,128]{2,1,0:T(8,128)}, f32[112,128]{1,0:T(8,128)}, f32[112,128]{1,0:T(8,128)}, f32[112,128]{1,0:T(8,128)}, /*index=5*/f32[128,128]{1,0:T(8,128)}) custom-call(f32[111,64,128]{2,1,0:T(8,128)} %bitcast.7, f32[64,128]{1,0:T(8,128)} %t_hbm.1, f32[111,111]{1,0:T(8,128)} %r_hbm.3), custom_call_target="tpu_custom_call" | custom-call | flops 1000000000 | bytes 11000000 | tf_op jit(solution)/shard_map/spread/pallas_call | solution.py:455
  6.7 0.8 %collective-permute-start = (f32[112,128]{1,0:T(8,128)}, f32[112,128]{1,0:T(8,128)S(1)}, u32[]{:S(2)}, u32[]{:S(2)}) collective-permute-start(f32[112,128]{1,0:T(8,128)} %get-tuple-element.13), channel_id=1, source_target_pairs={{0,4},{4,0},{8,12},{12,8},{16,20},{20,16},{24,28},{28,24},{32,36},... | collective-permute-start | bytes 172040 | tf_op jit(solution)/shard_map/ppermute | solution.py:479
  7.4 2.7 %collective-permute-start.1 = (f32[112,128]{1,0:T(8,128)}, f32[112,128]{1,0:T(8,128)S(1)}, u32[]{:S(2)}, u32[]{:S(2)}) collective-permute-start(f32[112,128]{1,0:T(8,128)} %get-tuple-element.14), channel_id=1, source_target_pairs={{4,8},{8,4},{12,16},{16,12},{20,24},{24,20},{28,32},{32,28},{36,40... | collective-permute-start | bytes 172040 | tf_op jit(solution)/shard_map/ppermute | solution.py:479
  10.2 1.9 %collective-permute-start.3 = (f32[112,128]{1,0:T(8,128)}, f32[112,128]{1,0:T(8,128)S(1)}, u32[]{:S(2)}, u32[]{:S(2)}) collective-permute-start(f32[112,128]{1,0:T(8,128)} %get-tuple-element.15.cols_hbm), channel_id=1, source_target_pairs={{1,2},{2,1},{5,6},{6,5},{9,10},{10,9},{13,14},{14,13},{17,18},{18,... | collective-permute-start | bytes 172040 | tf_op jit(solution)/shard_map/ppermute | solution.py:479
  12.1 0.2 collective-permute-start.2
  12.3 9.8 %all-to-all-start = ((f32[128,1,128]{2,1,0:T(1,128)}), f32[128,1,128]{2,1,0:T(1,128)S(1)}, u32[]{:S(2)}, u32[]{:S(2)}) async-start(f32[128,1,128]{2,1,0:T(1,128)} %bitcast.8), calls=%async_computation | async-start | bytes 131072 | tf_op jit(solution)/shard_map/all_to_all | solution.py:481
  22.1 0.0 collective-permute-done.even_hbm
  22.1 0.0 copy-start.1
  22.1 0.0 collective-permute-done.1.odd_hbm
  22.1 0.0 copy-start.2
  22.1 0.0 collective-permute-done.3.cross_hbm
  22.1 0.0 copy-start.3
  22.1 0.0 collective-permute-done.2.pair_hbm
  22.1 0.0 copy-start.4
  22.1 0.5 copy-done.1
  22.7 0.0 copy-done.2
  22.7 0.0 copy-done.3
  22.7 0.0 copy-done.4
  22.8 9.5 %flux.1.s_hbm = f32[64,112,128]{2,1,0:T(8,128)} custom-call(f32[64,112,128]{2,1,0:T(8,128)} %get-tuple-element.11.c_hbm, f32[64,112,128]{2,1,0:T(8,128)} %get-tuple-element.12.d_hbm, f32[112,128]{1,0:T(8,128)} %copy-done.1, f32[112,128]{1,0:T(8,128)} %copy-done.2, f32[112,128]{1,0:T(8,128)} %copy-done.4, f32[112,128]{1,0:T(8,128)} %copy-done.3, ...), custom_call_target="tpu_custom_call" | custom-call | flops 1000000000 | bytes 11000000 | tf_op jit(solution)/shard_map/flux/pallas_call | solution.py:487
  32.3 0.0 all-to-all-done
  32.3 0.0 copy-start
  32.3 0.6 %copy-done = f32[128,1,128]{2,1,0:T(1,128)} copy-done((f32[128,1,128]{2,1,0:T(1,128)}, f32[128,1,128]{2,1,0:T(1,128)S(1)}, u32[]{:S(2)}) %copy-start) | copy-done | bytes 65560
  32.9 25.4 %advance.1 = (f32[111,64,128]{2,1,0:T(8,128)}, f32[64,128]{1,0:T(8,128)}) custom-call(s32[64]{0:T(128)} %bitcast.10, f32[128,128]{1,0:T(8,128)} %bitcast.9, f32[64,112,128]{2,1,0:T(8,128)} %get-tuple-element.11.c_hbm, f32[64,112,128]{2,1,0:T(8,128)} %flux.1.s_hbm, f32[784]{0:T(1024)} %a_hbm.1, f32[784,111]{1,0:T(8,128)} %k_hbm.1, f32[784]{0:T(1024)} %e_hbm.1, ...), custom_call_target="tpu_custom_call" | custom-call | flops 20000000000 | bytes 11000000 | tf_op jit(solution)/shard_map/advance/pallas_call | solution.py:504
Async XLA Ops:
  6.7 15.4 %collective-permute-start = (f32[112,128]{1,0:T(8,128)}, f32[112,128]{1,0:T(8,128)S(1)}, u32[]{:S(2)}, u32[]{:S(2)}) collective-permute-start(f32[112,128]{1,0:T(8,128)} %get-tuple-element.13), channel_id=1, source_target_pairs={{0,4},{4,0},{8,12},{12,8},{16,20},{20,16},{24,28},{28,24},{32,36},... | collective-permute-start | bytes 172040 | tf_op jit(solution)/shard_map/ppermute | solution.py:479
  7.4 14.7 %collective-permute-start.1 = (f32[112,128]{1,0:T(8,128)}, f32[112,128]{1,0:T(8,128)S(1)}, u32[]{:S(2)}, u32[]{:S(2)}) collective-permute-start(f32[112,128]{1,0:T(8,128)} %get-tuple-element.14), channel_id=1, source_target_pairs={{4,8},{8,4},{12,16},{16,12},{20,24},{24,20},{28,32},{32,28},{36,40... | collective-permute-start | bytes 172040 | tf_op jit(solution)/shard_map/ppermute | solution.py:479
  10.2 11.9 %collective-permute-start.3 = (f32[112,128]{1,0:T(8,128)}, f32[112,128]{1,0:T(8,128)S(1)}, u32[]{:S(2)}, u32[]{:S(2)}) collective-permute-start(f32[112,128]{1,0:T(8,128)} %get-tuple-element.15.cols_hbm), channel_id=1, source_target_pairs={{1,2},{2,1},{5,6},{6,5},{9,10},{10,9},{13,14},{14,13},{17,18},{18,... | collective-permute-start | bytes 172040 | tf_op jit(solution)/shard_map/ppermute | solution.py:479
  12.1 10.0 %collective-permute-start.2 = (f32[112,128]{1,0:T(8,128)}, f32[112,128]{1,0:T(8,128)S(1)}, u32[]{:S(2)}, u32[]{:S(2)}) collective-permute-start(f32[112,128]{1,0:T(8,128)} %get-tuple-element.15.cols_hbm), channel_id=1, source_target_pairs={{0,1},{1,0},{2,3},{3,2},{4,5},{5,4},{6,7},{7,6},{8,9},{9,8},{10,11... | collective-permute-start | bytes 172040 | tf_op jit(solution)/shard_map/ppermute | solution.py:479
  12.3 20.0 %all-to-all-start = ((f32[128,1,128]{2,1,0:T(1,128)}), f32[128,1,128]{2,1,0:T(1,128)S(1)}, u32[]{:S(2)}, u32[]{:S(2)}) async-start(f32[128,1,128]{2,1,0:T(1,128)} %bitcast.8), calls=%async_computation | async-start | bytes 131072 | tf_op jit(solution)/shard_map/all_to_all | solution.py:481
  22.1 0.6 %copy-start.1 = (f32[112,128]{1,0:T(8,128)}, f32[112,128]{1,0:T(8,128)S(1)}, u32[]{:S(2)}) copy-start(f32[112,128]{1,0:T(8,128)S(1)} %collective-permute-done.even_hbm) | copy-start | bytes 172036
  22.1 0.6 %copy-start.2 = (f32[112,128]{1,0:T(8,128)}, f32[112,128]{1,0:T(8,128)S(1)}, u32[]{:S(2)}) copy-start(f32[112,128]{1,0:T(8,128)S(1)} %collective-permute-done.1.odd_hbm) | copy-start | bytes 172036
  22.1 0.6 %copy-start.3 = (f32[112,128]{1,0:T(8,128)}, f32[112,128]{1,0:T(8,128)S(1)}, u32[]{:S(2)}) copy-start(f32[112,128]{1,0:T(8,128)S(1)} %collective-permute-done.3.cross_hbm) | copy-start | bytes 172036
  22.1 0.6 %copy-start.4 = (f32[112,128]{1,0:T(8,128)}, f32[112,128]{1,0:T(8,128)S(1)}, u32[]{:S(2)}) copy-start(f32[112,128]{1,0:T(8,128)S(1)} %collective-permute-done.2.pair_hbm) | copy-start | bytes 172036
  32.3 0.6 %copy-start = (f32[128,1,128]{2,1,0:T(1,128)}, f32[128,1,128]{2,1,0:T(1,128)S(1)}, u32[]{:S(2)}) copy-start(f32[128,1,128]{2,1,0:T(1,128)S(1)} %all-to-all-done) | copy-start | bytes 196612

commit v3 on v2

--- a/solution.py
+++ b/solution.py
@@ -24,7 +24,7 @@
 STREAMS = 2
 SPAN = 784
 CHUNK = 8
-HALF = 4
+HALF = 16
 
 
 def split2(value):
@@ -213,16 +213,18 @@
         value = ref[pl.ds(base, HALF)].reshape(HALF * padded, LANES)
         return mxu(jnp.concatenate(split2(value), axis=1), step_ref[which])
 
-    wait_in(0)
+    for i in range(HALF // CHUNK):
+        wait_in(i)
     gap_ref[...] = (d_ref[0] + outer[:, 0:LANES]) * (c_ref[0] - above)
 
     @pl.loop(0, row_count // HALF)
     def _(part):
         base = part * HALF
 
-        @pl.when(jnp.logical_and(part % 2 == 1, part < row_count // HALF - 1))
+        @pl.when(part < row_count // HALF - 1)
         def _():
-            wait_in(part // 2 + 1)
+            for n in range(HALF // CHUNK):
+                wait_in((part + 1) * (HALF // CHUNK) + n)
 
         change = beside_of(c_ref, base, 0)
         total = beside_of(d_ref, base, 1)
@@ -238,10 +240,8 @@
             gap = later
         gap_ref[...] = gap
 
-        @pl.when(part % 2 == 1)
-        def _():
-            done = pl.ds((part // 2) * CHUNK, CHUNK)
-            pltpu.make_async_copy(s_ref.at[done], s_hbm.at[done], out_sem).start()
+        done = pl.ds(base, HALF)
+        pltpu.make_async_copy(s_ref.at[done], s_hbm.at[done], out_sem).start()
 
     pltpu.make_async_copy(s_ref, s_hbm, out_sem).wait()
 
@@ -302,7 +302,7 @@
         order_ref[found] = x
         return found + flag_ref[x]
 
-    live = lax.fori_loop(0, row_count, gather, jnp.int32(0))
+    live = lax.fori_loop(0, row_count, gather, jnp.int32(0), unroll=16)
     order_ref[live] = row_count
 
     for copy in small:

time: 59 us -> 57.1 us (0.968)
  the two profiles are of different devices: /device:TPU:85 before, /device:TPU:37 now
where the time goes in v3:
time: 57.1 us; the launch traced here: 56.7 us
  Pallas kernels  39.1 us (68%)
  starting transfers between devices  15.6 us (27%)
  local copies, waits for them, and re-layouts  1.23 us (2%)
  between operations  0.76 us (1%)
    pallas_call x1, Pallas kernels, per_device(): pl.pallas_call(functools.partial(advance_kernel, species, reactions), in_...  25.1 us
    all_to_all x1, starting transfers between devices, per_device(): peaks = lax.all_to_all(peak, FLOW_CHEM, 0, 0, tiled=True)  8.52 us
    pallas_call x1, Pallas kernels, per_device(): pl.pallas_call(flux_kernel, in_specs=[far] * 8, out_specs=far, out_shape=...  7.93 us
    ppermute x4, starting transfers between devices, swap(): return lax.ppermute(value, axis, pairs)  7.11 us
    pallas_call x1, Pallas kernels, per_device(): pl.pallas_call(functools.partial(spread_kernel, species), in_specs=[far,...  6.03 us
    unnamed x10, local copies, waits for them, and re-layouts  1.23 us
  transfers between devices with their start and end apart: 5, of which 0 were waited for; matrix products, arithmetic and copies ran while one was open for 0% of the time, Pallas kernels for 14%

profile of v3, /device:TPU:37, one launch (start us, length us, event | category | flops | bytes accessed | tf_op | source)
XLA Modules:
  0.0 56.7 jit_solution(16595429111581551327)
XLA Ops:
  0.6 6.0 %spread.1 = (f32[64,112,128]{2,1,0:T(8,128)}, f32[64,112,128]{2,1,0:T(8,128)}, f32[112,128]{1,0:T(8,128)}, f32[112,128]{1,0:T(8,128)}, f32[112,128]{1,0:T(8,128)}, /*index=5*/f32[128,128]{1,0:T(8,128)}) custom-call(f32[111,64,128]{2,1,0:T(8,128)} %bitcast.7, f32[64,128]{1,0:T(8,128)} %t_hbm.1, f32[111,111]{1,0:T(8,128)} %r_hbm.3), custom_call_target="tpu_custom_call" | custom-call | flops 1000000000 | bytes 11000000 | tf_op jit(solution)/shard_map/spread/pallas_call | solution.py:455
  6.7 0.8 %collective-permute-start = (f32[112,128]{1,0:T(8,128)}, f32[112,128]{1,0:T(8,128)S(1)}, u32[]{:S(2)}, u32[]{:S(2)}) collective-permute-start(f32[112,128]{1,0:T(8,128)} %get-tuple-element.13), channel_id=1, source_target_pairs={{0,4},{4,0},{8,12},{12,8},{16,20},{20,16},{24,28},{28,24},{32,36},... | collective-permute-start | bytes 172040 | tf_op jit(solution)/shard_map/ppermute | solution.py:479
  7.4 2.7 %collective-permute-start.1 = (f32[112,128]{1,0:T(8,128)}, f32[112,128]{1,0:T(8,128)S(1)}, u32[]{:S(2)}, u32[]{:S(2)}) collective-permute-start(f32[112,128]{1,0:T(8,128)} %get-tuple-element.14), channel_id=1, source_target_pairs={{4,8},{8,4},{12,16},{16,12},{20,24},{24,20},{28,32},{32,28},{36,40... | collective-permute-start | bytes 172040 | tf_op jit(solution)/shard_map/ppermute | solution.py:479
  10.2 3.6 %collective-permute-start.3 = (f32[112,128]{1,0:T(8,128)}, f32[112,128]{1,0:T(8,128)S(1)}, u32[]{:S(2)}, u32[]{:S(2)}) collective-permute-start(f32[112,128]{1,0:T(8,128)} %get-tuple-element.15.cols_hbm), channel_id=1, source_target_pairs={{1,2},{2,1},{5,6},{6,5},{9,10},{10,9},{13,14},{14,13},{17,18},{18,... | collective-permute-start | bytes 172040 | tf_op jit(solution)/shard_map/ppermute | solution.py:479
  13.7 0.1 collective-permute-start.2
  13.8 8.5 %all-to-all-start = ((f32[128,1,128]{2,1,0:T(1,128)}), f32[128,1,128]{2,1,0:T(1,128)S(1)}, u32[]{:S(2)}, u32[]{:S(2)}) async-start(f32[128,1,128]{2,1,0:T(1,128)} %bitcast.8), calls=%async_computation | async-start | bytes 131072 | tf_op jit(solution)/shard_map/all_to_all | solution.py:481
  22.3 0.0 collective-permute-done.even_hbm
  22.3 0.0 copy-start.1
  22.4 0.0 collective-permute-done.1.odd_hbm
  22.4 0.0 copy-start.2
  22.4 0.0 collective-permute-done.3.cross_hbm
  22.4 0.0 copy-start.3
  22.4 0.0 collective-permute-done.2.pair_hbm
  22.4 0.0 copy-start.4
  22.4 0.5 copy-done.1
  23.0 0.0 copy-done.2
  23.0 0.0 copy-done.3
  23.0 0.0 copy-done.4
  23.0 7.9 %flux.1.s_hbm = f32[64,112,128]{2,1,0:T(8,128)} custom-call(f32[64,112,128]{2,1,0:T(8,128)} %get-tuple-element.11.c_hbm, f32[64,112,128]{2,1,0:T(8,128)} %get-tuple-element.12.d_hbm, f32[112,128]{1,0:T(8,128)} %copy-done.1, f32[112,128]{1,0:T(8,128)} %copy-done.2, f32[112,128]{1,0:T(8,128)} %copy-done.4, f32[112,128]{1,0:T(8,128)} %copy-done.3, ...), custom_call_target="tpu_custom_call" | custom-call | flops 1000000000 | bytes 11000000 | tf_op jit(solution)/shard_map/flux/pallas_call | solution.py:487
  31.0 0.0 all-to-all-done
  31.0 0.0 copy-start
  31.0 0.6 %copy-done = f32[128,1,128]{2,1,0:T(1,128)} copy-done((f32[128,1,128]{2,1,0:T(1,128)}, f32[128,1,128]{2,1,0:T(1,128)S(1)}, u32[]{:S(2)}) %copy-start) | copy-done | bytes 65560
  31.6 25.1 %advance.1 = (f32[111,64,128]{2,1,0:T(8,128)}, f32[64,128]{1,0:T(8,128)}) custom-call(s32[64]{0:T(128)} %bitcast.10, f32[128,128]{1,0:T(8,128)} %bitcast.9, f32[64,112,128]{2,1,0:T(8,128)} %get-tuple-element.11.c_hbm, f32[64,112,128]{2,1,0:T(8,128)} %flux.1.s_hbm, f32[784]{0:T(1024)} %a_hbm.1, f32[784,111]{1,0:T(8,128)} %k_hbm.1, f32[784]{0:T(1024)} %e_hbm.1, ...), custom_call_target="tpu_custom_call" | custom-call | flops 20000000000 | bytes 11000000 | tf_op jit(solution)/shard_map/advance/pallas_call | solution.py:504
Async XLA Ops:
  6.7 15.7 %collective-permute-start = (f32[112,128]{1,0:T(8,128)}, f32[112,128]{1,0:T(8,128)S(1)}, u32[]{:S(2)}, u32[]{:S(2)}) collective-permute-start(f32[112,128]{1,0:T(8,128)} %get-tuple-element.13), channel_id=1, source_target_pairs={{0,4},{4,0},{8,12},{12,8},{16,20},{20,16},{24,28},{28,24},{32,36},... | collective-permute-start | bytes 172040 | tf_op jit(solution)/shard_map/ppermute | solution.py:479
  7.4 14.9 %collective-permute-start.1 = (f32[112,128]{1,0:T(8,128)}, f32[112,128]{1,0:T(8,128)S(1)}, u32[]{:S(2)}, u32[]{:S(2)}) collective-permute-start(f32[112,128]{1,0:T(8,128)} %get-tuple-element.14), channel_id=1, source_target_pairs={{4,8},{8,4},{12,16},{16,12},{20,24},{24,20},{28,32},{32,28},{36,40... | collective-permute-start | bytes 172040 | tf_op jit(solution)/shard_map/ppermute | solution.py:479
  10.2 12.2 %collective-permute-start.3 = (f32[112,128]{1,0:T(8,128)}, f32[112,128]{1,0:T(8,128)S(1)}, u32[]{:S(2)}, u32[]{:S(2)}) collective-permute-start(f32[112,128]{1,0:T(8,128)} %get-tuple-element.15.cols_hbm), channel_id=1, source_target_pairs={{1,2},{2,1},{5,6},{6,5},{9,10},{10,9},{13,14},{14,13},{17,18},{18,... | collective-permute-start | bytes 172040 | tf_op jit(solution)/shard_map/ppermute | solution.py:479
  13.7 8.7 %collective-permute-start.2 = (f32[112,128]{1,0:T(8,128)}, f32[112,128]{1,0:T(8,128)S(1)}, u32[]{:S(2)}, u32[]{:S(2)}) collective-permute-start(f32[112,128]{1,0:T(8,128)} %get-tuple-element.15.cols_hbm), channel_id=1, source_target_pairs={{0,1},{1,0},{2,3},{3,2},{4,5},{5,4},{6,7},{7,6},{8,9},{9,8},{10,11... | collective-permute-start | bytes 172040 | tf_op jit(solution)/shard_map/ppermute | solution.py:479
  13.8 17.2 %all-to-all-start = ((f32[128,1,128]{2,1,0:T(1,128)}), f32[128,1,128]{2,1,0:T(1,128)S(1)}, u32[]{:S(2)}, u32[]{:S(2)}) async-start(f32[128,1,128]{2,1,0:T(1,128)} %bitcast.8), calls=%async_computation | async-start | bytes 131072 | tf_op jit(solution)/shard_map/all_to_all | solution.py:481
  22.3 0.6 %copy-start.1 = (f32[112,128]{1,0:T(8,128)}, f32[112,128]{1,0:T(8,128)S(1)}, u32[]{:S(2)}) copy-start(f32[112,128]{1,0:T(8,128)S(1)} %collective-permute-done.even_hbm) | copy-start | bytes 172036
  22.4 0.6 %copy-start.2 = (f32[112,128]{1,0:T(8,128)}, f32[112,128]{1,0:T(8,128)S(1)}, u32[]{:S(2)}) copy-start(f32[112,128]{1,0:T(8,128)S(1)} %collective-permute-done.1.odd_hbm) | copy-start | bytes 172036
  22.4 0.6 %copy-start.3 = (f32[112,128]{1,0:T(8,128)}, f32[112,128]{1,0:T(8,128)S(1)}, u32[]{:S(2)}) copy-start(f32[112,128]{1,0:T(8,128)S(1)} %collective-permute-done.3.cross_hbm) | copy-start | bytes 172036
  22.4 0.6 %copy-start.4 = (f32[112,128]{1,0:T(8,128)}, f32[112,128]{1,0:T(8,128)S(1)}, u32[]{:S(2)}) copy-start(f32[112,128]{1,0:T(8,128)S(1)} %collective-permute-done.2.pair_hbm) | copy-start | bytes 172036
  31.0 0.6 %copy-start = (f32[128,1,128]{2,1,0:T(1,128)}, f32[128,1,128]{2,1,0:T(1,128)S(1)}, u32[]{:S(2)}) copy-start(f32[128,1,128]{2,1,0:T(1,128)S(1)} %all-to-all-done) | copy-start | bytes 196612

commit v4 on v3

--- a/solution.py
+++ b/solution.py
@@ -24,6 +24,7 @@
 STREAMS = 2
 SPAN = 784
 CHUNK = 8
+TOGETHER = 2
 HALF = 16
 
 
@@ -94,12 +95,17 @@
     stack_inverse(rs_ref, square)
     heat_in.wait()
 
-    def send(buf, hbm, i):
-        here = pl.ds(i * CHUNK, CHUNK)
-        pltpu.make_async_copy(buf.at[here], hbm.at[here], out_sem).start()
+    def some(step, peak):
+        for n in range(TOGETHER):
+            chunk_in(step * TOGETHER + n).wait()
+        for n in range(TOGETHER):
+            peak = chunk(step * TOGETHER + n, peak)
+        rows = pl.ds(step * (TOGETHER * CHUNK), TOGETHER * CHUNK)
+        pltpu.make_async_copy(c_buf.at[rows], c_hbm.at[rows], out_sem).start()
+        pltpu.make_async_copy(d_buf.at[rows], d_hbm.at[rows], out_sem).start()
+        return peak
 
     def chunk(i, peak):
-        chunk_in(i).wait()
         flat = x_buf.at[i].reshape(species * CHUNK, LANES)
         base = i * CHUNK
         first = jnp.zeros((padded, LANES), F32)
@@ -127,11 +133,9 @@
         here = lane // CHUNK == i
         first_col[...] = jnp.where(here, pltpu.roll(first, base, 1), first_col[...])
         last_col[...] = jnp.where(here, pltpu.roll(last, base + 1, 1), last_col[...])
-        send(c_buf, c_hbm, i)
-        send(d_buf, d_hbm, i)
         return peak
 
-    peak = lax.fori_loop(0, chunks, chunk, jnp.zeros((padded, LANES), F32))
+    peak = lax.fori_loop(0, chunks // TOGETHER, some, jnp.zeros((padded, LANES), F32))
     best = jnp.max(jnp.max(peak, axis=0, keepdims=True), axis=1, keepdims=True)
     peak_ref[...] = jnp.broadcast_to(best, peak_ref.shape)
     cols_ref[...] = jnp.where(lane < 64, first_col[...], pltpu.roll(last_col[...], 64, 1))
@@ -333,18 +337,23 @@
         pltpu.make_async_copy(o_ref.at[i], out_hbm.at[:, pl.ds(i * CHUNK, CHUNK)], out_sem).start()
         return 0
 
-    def quiet_rows(i, _):
-        for copy in chunk_in(i):
-            copy.wait()
+    def quiet_pair(step, _):
+        for n in (0, 1):
+            for copy in chunk_in(2 * step + n):
+                copy.wait()
+        quiet_rows(2 * step)
+        quiet_rows(2 * step + 1)
+        return 0
+
+    def quiet_rows(i):
         for r in range(CHUNK):
             x = i * CHUNK + r
             value = c_ref[x] + half_ref[...] * s_ref[x]
             c_ref[x, 0:species] = value[0:species]
             flat_out[pl.ds(i * (CHUNK * species) + r, species, stride=CHUNK), :] = value[0:species]
             heat_ref[pl.ds(x, 1), :] = c_ref[x, padded - 1 : padded]
-        return 0
-
-    lax.fori_loop(0, chunks, quiet_rows, 0)
+
+    lax.fori_loop(0, chunks // 2, quiet_pair, 0)
 
     ceiling = RATE_CEILING * LOG2E
 

time: 57.1 us -> 56.9 us (level)
  the two profiles are of different devices: /device:TPU:37 before, /device:TPU:25 now
where the time goes in v4:
time: 56.9 us; the launch traced here: 56.6 us
  Pallas kernels  38.9 us (68%)
  starting transfers between devices  15.7 us (28%)
  local copies, waits for them, and re-layouts  1.23 us (2%)
  between operations  0.75 us (1%)
    pallas_call x1, Pallas kernels, per_device(): pl.pallas_call(functools.partial(advance_kernel, species, reactions), in_...  25.1 us
    ppermute x4, starting transfers between devices, swap(): return lax.ppermute(value, axis, pairs)  9.02 us
    pallas_call x1, Pallas kernels, per_device(): pl.pallas_call(flux_kernel, in_specs=[far] * 8, out_specs=far, out_shape=...  7.93 us
    all_to_all x1, starting transfers between devices, per_device(): peaks = lax.all_to_all(peak, FLOW_CHEM, 0, 0, tiled=True)  6.69 us
    pallas_call x1, Pallas kernels, per_device(): pl.pallas_call(functools.partial(spread_kernel, species), in_specs=[far,...  5.82 us
    unnamed x10, local copies, waits for them, and re-layouts  1.23 us
  transfers between devices with their start and end apart: 5, of which 0 were waited for; matrix products, arithmetic and copies ran while one was open for 0% of the time, Pallas kernels for 14%

profile of v4, /device:TPU:25, one launch (start us, length us, event | category | flops | bytes accessed | tf_op | source)
XLA Modules:
  0.0 56.6 jit_solution(8209467946310264145)
XLA Ops:
  0.6 5.8 %spread.1 = (f32[64,112,128]{2,1,0:T(8,128)}, f32[64,112,128]{2,1,0:T(8,128)}, f32[112,128]{1,0:T(8,128)}, f32[112,128]{1,0:T(8,128)}, f32[112,128]{1,0:T(8,128)}, /*index=5*/f32[128,128]{1,0:T(8,128)}) custom-call(f32[111,64,128]{2,1,0:T(8,128)} %bitcast.7, f32[64,128]{1,0:T(8,128)} %t_hbm.1, f32[111,111]{1,0:T(8,128)} %r_hbm.3), custom_call_target="tpu_custom_call" | custom-call | flops 1000000000 | bytes 11000000 | tf_op jit(solution)/shard_map/spread/pallas_call | solution.py:464
  6.5 0.7 %collective-permute-start = (f32[112,128]{1,0:T(8,128)}, f32[112,128]{1,0:T(8,128)S(1)}, u32[]{:S(2)}, u32[]{:S(2)}) collective-permute-start(f32[112,128]{1,0:T(8,128)} %get-tuple-element.13), channel_id=1, source_target_pairs={{0,4},{4,0},{8,12},{12,8},{16,20},{20,16},{24,28},{28,24},{32,36},... | collective-permute-start | bytes 172040 | tf_op jit(solution)/shard_map/ppermute | solution.py:488
  7.2 3.0 %collective-permute-start.1 = (f32[112,128]{1,0:T(8,128)}, f32[112,128]{1,0:T(8,128)S(1)}, u32[]{:S(2)}, u32[]{:S(2)}) collective-permute-start(f32[112,128]{1,0:T(8,128)} %get-tuple-element.14), channel_id=1, source_target_pairs={{4,8},{8,4},{12,16},{16,12},{20,24},{24,20},{28,32},{32,28},{36,40... | collective-permute-start | bytes 172040 | tf_op jit(solution)/shard_map/ppermute | solution.py:488
  10.2 0.7 %collective-permute-start.3 = (f32[112,128]{1,0:T(8,128)}, f32[112,128]{1,0:T(8,128)S(1)}, u32[]{:S(2)}, u32[]{:S(2)}) collective-permute-start(f32[112,128]{1,0:T(8,128)} %get-tuple-element.15.cols_hbm), channel_id=1, source_target_pairs={{1,2},{2,1},{5,6},{6,5},{9,10},{10,9},{13,14},{14,13},{17,18},{18,... | collective-permute-start | bytes 172040 | tf_op jit(solution)/shard_map/ppermute | solution.py:488
  10.9 4.6 %collective-permute-start.2 = (f32[112,128]{1,0:T(8,128)}, f32[112,128]{1,0:T(8,128)S(1)}, u32[]{:S(2)}, u32[]{:S(2)}) collective-permute-start(f32[112,128]{1,0:T(8,128)} %get-tuple-element.15.cols_hbm), channel_id=1, source_target_pairs={{0,1},{1,0},{2,3},{3,2},{4,5},{5,4},{6,7},{7,6},{8,9},{9,8},{10,11... | collective-permute-start | bytes 172040 | tf_op jit(solution)/shard_map/ppermute | solution.py:488
  15.5 6.7 %all-to-all-start = ((f32[128,1,128]{2,1,0:T(1,128)}), f32[128,1,128]{2,1,0:T(1,128)S(1)}, u32[]{:S(2)}, u32[]{:S(2)}) async-start(f32[128,1,128]{2,1,0:T(1,128)} %bitcast.8), calls=%async_computation | async-start | bytes 131072 | tf_op jit(solution)/shard_map/all_to_all | solution.py:490
  22.2 0.0 collective-permute-done.even_hbm
  22.2 0.0 copy-start.1
  22.2 0.0 collective-permute-done.1.odd_hbm
  22.2 0.0 copy-start.2
  22.2 0.0 collective-permute-done.3.cross_hbm
  22.2 0.0 copy-start.3
  22.3 0.0 collective-permute-done.2.pair_hbm
  22.3 0.0 copy-start.4
  22.3 0.5 copy-done.1
  22.8 0.0 copy-done.2
  22.8 0.0 copy-done.3
  22.9 0.0 copy-done.4
  22.9 7.9 %flux.1.s_hbm = f32[64,112,128]{2,1,0:T(8,128)} custom-call(f32[64,112,128]{2,1,0:T(8,128)} %get-tuple-element.11.c_hbm, f32[64,112,128]{2,1,0:T(8,128)} %get-tuple-element.12.d_hbm, f32[112,128]{1,0:T(8,128)} %copy-done.1, f32[112,128]{1,0:T(8,128)} %copy-done.2, f32[112,128]{1,0:T(8,128)} %copy-done.4, f32[112,128]{1,0:T(8,128)} %copy-done.3, ...), custom_call_target="tpu_custom_call" | custom-call | flops 1000000000 | bytes 11000000 | tf_op jit(solution)/shard_map/flux/pallas_call | solution.py:496
  30.8 0.0 all-to-all-done
  30.8 0.0 copy-start
  30.8 0.6 %copy-done = f32[128,1,128]{2,1,0:T(1,128)} copy-done((f32[128,1,128]{2,1,0:T(1,128)}, f32[128,1,128]{2,1,0:T(1,128)S(1)}, u32[]{:S(2)}) %copy-start) | copy-done | bytes 65560
  31.5 25.1 %advance.1 = (f32[111,64,128]{2,1,0:T(8,128)}, f32[64,128]{1,0:T(8,128)}) custom-call(s32[64]{0:T(128)} %bitcast.10, f32[128,128]{1,0:T(8,128)} %bitcast.9, f32[64,112,128]{2,1,0:T(8,128)} %get-tuple-element.11.c_hbm, f32[64,112,128]{2,1,0:T(8,128)} %flux.1.s_hbm, f32[784]{0:T(1024)} %a_hbm.1, f32[784,111]{1,0:T(8,128)} %k_hbm.1, f32[784]{0:T(1024)} %e_hbm.1, ...), custom_call_target="tpu_custom_call" | custom-call | flops 20000000000 | bytes 11000000 | tf_op jit(solution)/shard_map/advance/pallas_call | solution.py:513
Async XLA Ops:
  6.5 15.7 %collective-permute-start = (f32[112,128]{1,0:T(8,128)}, f32[112,128]{1,0:T(8,128)S(1)}, u32[]{:S(2)}, u32[]{:S(2)}) collective-permute-start(f32[112,128]{1,0:T(8,128)} %get-tuple-element.13), channel_id=1, source_target_pairs={{0,4},{4,0},{8,12},{12,8},{16,20},{20,16},{24,28},{28,24},{32,36},... | collective-permute-start | bytes 172040 | tf_op jit(solution)/shard_map/ppermute | solution.py:488
  7.2 15.0 %collective-permute-start.1 = (f32[112,128]{1,0:T(8,128)}, f32[112,128]{1,0:T(8,128)S(1)}, u32[]{:S(2)}, u32[]{:S(2)}) collective-permute-start(f32[112,128]{1,0:T(8,128)} %get-tuple-element.14), channel_id=1, source_target_pairs={{4,8},{8,4},{12,16},{16,12},{20,24},{24,20},{28,32},{32,28},{36,40... | collective-permute-start | bytes 172040 | tf_op jit(solution)/shard_map/ppermute | solution.py:488
  10.2 12.0 %collective-permute-start.3 = (f32[112,128]{1,0:T(8,128)}, f32[112,128]{1,0:T(8,128)S(1)}, u32[]{:S(2)}, u32[]{:S(2)}) collective-permute-start(f32[112,128]{1,0:T(8,128)} %get-tuple-element.15.cols_hbm), channel_id=1, source_target_pairs={{1,2},{2,1},{5,6},{6,5},{9,10},{10,9},{13,14},{14,13},{17,18},{18,... | collective-permute-start | bytes 172040 | tf_op jit(solution)/shard_map/ppermute | solution.py:488
  10.9 11.4 %collective-permute-start.2 = (f32[112,128]{1,0:T(8,128)}, f32[112,128]{1,0:T(8,128)S(1)}, u32[]{:S(2)}, u32[]{:S(2)}) collective-permute-start(f32[112,128]{1,0:T(8,128)} %get-tuple-element.15.cols_hbm), channel_id=1, source_target_pairs={{0,1},{1,0},{2,3},{3,2},{4,5},{5,4},{6,7},{7,6},{8,9},{9,8},{10,11... | collective-permute-start | bytes 172040 | tf_op jit(solution)/shard_map/ppermute | solution.py:488
  15.5 15.3 %all-to-all-start = ((f32[128,1,128]{2,1,0:T(1,128)}), f32[128,1,128]{2,1,0:T(1,128)S(1)}, u32[]{:S(2)}, u32[]{:S(2)}) async-start(f32[128,1,128]{2,1,0:T(1,128)} %bitcast.8), calls=%async_computation | async-start | bytes 131072 | tf_op jit(solution)/shard_map/all_to_all | solution.py:490
  22.2 0.6 %copy-start.1 = (f32[112,128]{1,0:T(8,128)}, f32[112,128]{1,0:T(8,128)S(1)}, u32[]{:S(2)}) copy-start(f32[112,128]{1,0:T(8,128)S(1)} %collective-permute-done.even_hbm) | copy-start | bytes 172036
  22.2 0.6 %copy-start.2 = (f32[112,128]{1,0:T(8,128)}, f32[112,128]{1,0:T(8,128)S(1)}, u32[]{:S(2)}) copy-start(f32[112,128]{1,0:T(8,128)S(1)} %collective-permute-done.1.odd_hbm) | copy-start | bytes 172036
  22.2 0.6 %copy-start.3 = (f32[112,128]{1,0:T(8,128)}, f32[112,128]{1,0:T(8,128)S(1)}, u32[]{:S(2)}) copy-start(f32[112,128]{1,0:T(8,128)S(1)} %collective-permute-done.3.cross_hbm) | copy-start | bytes 172036
  22.3 0.6 %copy-start.4 = (f32[112,128]{1,0:T(8,128)}, f32[112,128]{1,0:T(8,128)S(1)}, u32[]{:S(2)}) copy-start(f32[112,128]{1,0:T(8,128)S(1)} %collective-permute-done.2.pair_hbm) | copy-start | bytes 172036
  30.8 0.6 %copy-start = (f32[128,1,128]{2,1,0:T(1,128)}, f32[128,1,128]{2,1,0:T(1,128)S(1)}, u32[]{:S(2)}) copy-start(f32[128,1,128]{2,1,0:T(1,128)S(1)} %all-to-all-done) | copy-start | bytes 196612

commit v5 on v4

--- a/solution.py
+++ b/solution.py
@@ -213,11 +213,15 @@
         for copy in chunk_in(i):
             copy.wait()
 
+    def wait_chunk(i, _):
+        wait_in(i)
+        return 0
+
     def beside_of(ref, base, which):
         value = ref[pl.ds(base, HALF)].reshape(HALF * padded, LANES)
         return mxu(jnp.concatenate(split2(value), axis=1), step_ref[which])
 
-    for i in range(HALF // CHUNK):
+    for i in range(HALF // CHUNK + 1):
         wait_in(i)
     gap_ref[...] = (d_ref[0] + outer[:, 0:LANES]) * (c_ref[0] - above)
 
@@ -225,10 +229,9 @@
     def _(part):
         base = part * HALF
 
-        @pl.when(part < row_count // HALF - 1)
-        def _():
-            for n in range(HALF // CHUNK):
-                wait_in((part + 1) * (HALF // CHUNK) + n)
+        ready = part * (HALF // CHUNK) + 1
+        fresh = jnp.where(part == 0, ready + HALF // CHUNK, ready)
+        lax.fori_loop(fresh, jnp.minimum(ready + HALF // CHUNK, chunks), wait_chunk, 0)
 
         change = beside_of(c_ref, base, 0)
         total = beside_of(d_ref, base, 1)

time: 56.9 us -> 57.3 us (level)
  the two profiles are of different devices: /device:TPU:25 before, /device:TPU:41 now
where the time goes in v5:
time: 57.3 us; the launch traced here: 56.5 us
  Pallas kernels  38.9 us (68%)
  starting transfers between devices  15.6 us (27%)
  local copies, waits for them, and re-layouts  1.23 us (2%)
  between operations  0.76 us (1%)
    pallas_call x1, Pallas kernels, per_device(): pl.pallas_call(functools.partial(advance_kernel, species, reactions), in_...  25.1 us
    all_to_all x1, starting transfers between devices, per_device(): peaks = lax.all_to_all(peak, FLOW_CHEM, 0, 0, tiled=True)  8.22 us
    pallas_call x1, Pallas kernels, per_device(): pl.pallas_call(flux_kernel, in_specs=[far] * 8, out_specs=far, out_shape=...  7.97 us
    ppermute x4, starting transfers between devices, swap(): return lax.ppermute(value, axis, pairs)  7.39 us
    pallas_call x1, Pallas kernels, per_device(): pl.pallas_call(functools.partial(spread_kernel, species), in_specs=[far,...  5.82 us
    unnamed x10, local copies, waits for them, and re-layouts  1.23 us
  transfers between devices with their start and end apart: 5, of which 0 were waited for; matrix products, arithmetic and copies ran while one was open for 0% of the time, Pallas kernels for 14%

profile of v5, /device:TPU:41, one launch (start us, length us, event | category | flops | bytes accessed | tf_op | source)
XLA Modules:
  0.0 56.5 jit_solution(11430391186737267909)
XLA Ops:
  0.6 5.8 %spread.1 = (f32[64,112,128]{2,1,0:T(8,128)}, f32[64,112,128]{2,1,0:T(8,128)}, f32[112,128]{1,0:T(8,128)}, f32[112,128]{1,0:T(8,128)}, f32[112,128]{1,0:T(8,128)}, /*index=5*/f32[128,128]{1,0:T(8,128)}) custom-call(f32[111,64,128]{2,1,0:T(8,128)} %bitcast.7, f32[64,128]{1,0:T(8,128)} %t_hbm.1, f32[111,111]{1,0:T(8,128)} %r_hbm.3), custom_call_target="tpu_custom_call" | custom-call | flops 1000000000 | bytes 11000000 | tf_op jit(solution)/shard_map/spread/pallas_call | solution.py:467
  6.5 0.7 %collective-permute-start = (f32[112,128]{1,0:T(8,128)}, f32[112,128]{1,0:T(8,128)S(1)}, u32[]{:S(2)}, u32[]{:S(2)}) collective-permute-start(f32[112,128]{1,0:T(8,128)} %get-tuple-element.13), channel_id=1, source_target_pairs={{0,4},{4,0},{8,12},{12,8},{16,20},{20,16},{24,28},{28,24},{32,36},... | collective-permute-start | bytes 172040 | tf_op jit(solution)/shard_map/ppermute | solution.py:491
  7.2 3.0 %collective-permute-start.1 = (f32[112,128]{1,0:T(8,128)}, f32[112,128]{1,0:T(8,128)S(1)}, u32[]{:S(2)}, u32[]{:S(2)}) collective-permute-start(f32[112,128]{1,0:T(8,128)} %get-tuple-element.14), channel_id=1, source_target_pairs={{4,8},{8,4},{12,16},{16,12},{20,24},{24,20},{28,32},{32,28},{36,40... | collective-permute-start | bytes 172040 | tf_op jit(solution)/shard_map/ppermute | solution.py:491
  10.2 3.5 %collective-permute-start.3 = (f32[112,128]{1,0:T(8,128)}, f32[112,128]{1,0:T(8,128)S(1)}, u32[]{:S(2)}, u32[]{:S(2)}) collective-permute-start(f32[112,128]{1,0:T(8,128)} %get-tuple-element.15.cols_hbm), channel_id=1, source_target_pairs={{1,2},{2,1},{5,6},{6,5},{9,10},{10,9},{13,14},{14,13},{17,18},{18,... | collective-permute-start | bytes 172040 | tf_op jit(solution)/shard_map/ppermute | solution.py:491
  13.8 0.1 collective-permute-start.2
  13.9 8.2 %all-to-all-start = ((f32[128,1,128]{2,1,0:T(1,128)}), f32[128,1,128]{2,1,0:T(1,128)S(1)}, u32[]{:S(2)}, u32[]{:S(2)}) async-start(f32[128,1,128]{2,1,0:T(1,128)} %bitcast.8), calls=%async_computation | async-start | bytes 131072 | tf_op jit(solution)/shard_map/all_to_all | solution.py:493
  22.1 0.0 collective-permute-done.even_hbm
  22.1 0.0 copy-start.1
  22.1 0.0 collective-permute-done.1.odd_hbm
  22.1 0.0 copy-start.2
  22.1 0.0 collective-permute-done.3.cross_hbm
  22.1 0.0 copy-start.3
  22.2 0.0 collective-permute-done.2.pair_hbm
  22.2 0.0 copy-start.4
  22.2 0.5 copy-done.1
  22.7 0.0 copy-done.2
  22.7 0.0 copy-done.3
  22.8 0.0 copy-done.4
  22.8 8.0 %flux.1.s_hbm = f32[64,112,128]{2,1,0:T(8,128)} custom-call(f32[64,112,128]{2,1,0:T(8,128)} %get-tuple-element.11.c_hbm, f32[64,112,128]{2,1,0:T(8,128)} %get-tuple-element.12.d_hbm, f32[112,128]{1,0:T(8,128)} %copy-done.1, f32[112,128]{1,0:T(8,128)} %copy-done.2, f32[112,128]{1,0:T(8,128)} %copy-done.4, f32[112,128]{1,0:T(8,128)} %copy-done.3, ...), custom_call_target="tpu_custom_call" | custom-call | flops 1000000000 | bytes 11000000 | tf_op jit(solution)/shard_map/flux/pallas_call | solution.py:499
  30.8 0.0 all-to-all-done
  30.8 0.0 copy-start
  30.8 0.6 %copy-done = f32[128,1,128]{2,1,0:T(1,128)} copy-done((f32[128,1,128]{2,1,0:T(1,128)}, f32[128,1,128]{2,1,0:T(1,128)S(1)}, u32[]{:S(2)}) %copy-start) | copy-done | bytes 65560
  31.4 25.1 %advance.1 = (f32[111,64,128]{2,1,0:T(8,128)}, f32[64,128]{1,0:T(8,128)}) custom-call(s32[64]{0:T(128)} %bitcast.10, f32[128,128]{1,0:T(8,128)} %bitcast.9, f32[64,112,128]{2,1,0:T(8,128)} %get-tuple-element.11.c_hbm, f32[64,112,128]{2,1,0:T(8,128)} %flux.1.s_hbm, f32[784]{0:T(1024)} %a_hbm.1, f32[784,111]{1,0:T(8,128)} %k_hbm.1, f32[784]{0:T(1024)} %e_hbm.1, ...), custom_call_target="tpu_custom_call" | custom-call | flops 20000000000 | bytes 11000000 | tf_op jit(solution)/shard_map/advance/pallas_call | solution.py:516
Async XLA Ops:
  6.5 15.6 %collective-permute-start = (f32[112,128]{1,0:T(8,128)}, f32[112,128]{1,0:T(8,128)S(1)}, u32[]{:S(2)}, u32[]{:S(2)}) collective-permute-start(f32[112,128]{1,0:T(8,128)} %get-tuple-element.13), channel_id=1, source_target_pairs={{0,4},{4,0},{8,12},{12,8},{16,20},{20,16},{24,28},{28,24},{32,36},... | collective-permute-start | bytes 172040 | tf_op jit(solution)/shard_map/ppermute | solution.py:491
  7.2 14.9 %collective-permute-start.1 = (f32[112,128]{1,0:T(8,128)}, f32[112,128]{1,0:T(8,128)S(1)}, u32[]{:S(2)}, u32[]{:S(2)}) collective-permute-start(f32[112,128]{1,0:T(8,128)} %get-tuple-element.14), channel_id=1, source_target_pairs={{4,8},{8,4},{12,16},{16,12},{20,24},{24,20},{28,32},{32,28},{36,40... | collective-permute-start | bytes 172040 | tf_op jit(solution)/shard_map/ppermute | solution.py:491
  10.2 11.9 %collective-permute-start.3 = (f32[112,128]{1,0:T(8,128)}, f32[112,128]{1,0:T(8,128)S(1)}, u32[]{:S(2)}, u32[]{:S(2)}) collective-permute-start(f32[112,128]{1,0:T(8,128)} %get-tuple-element.15.cols_hbm), channel_id=1, source_target_pairs={{1,2},{2,1},{5,6},{6,5},{9,10},{10,9},{13,14},{14,13},{17,18},{18,... | collective-permute-start | bytes 172040 | tf_op jit(solution)/shard_map/ppermute | solution.py:491
  13.8 8.4 %collective-permute-start.2 = (f32[112,128]{1,0:T(8,128)}, f32[112,128]{1,0:T(8,128)S(1)}, u32[]{:S(2)}, u32[]{:S(2)}) collective-permute-start(f32[112,128]{1,0:T(8,128)} %get-tuple-element.15.cols_hbm), channel_id=1, source_target_pairs={{0,1},{1,0},{2,3},{3,2},{4,5},{5,4},{6,7},{7,6},{8,9},{9,8},{10,11... | collective-permute-start | bytes 172040 | tf_op jit(solution)/shard_map/ppermute | solution.py:491
  13.9 16.9 %all-to-all-start = ((f32[128,1,128]{2,1,0:T(1,128)}), f32[128,1,128]{2,1,0:T(1,128)S(1)}, u32[]{:S(2)}, u32[]{:S(2)}) async-start(f32[128,1,128]{2,1,0:T(1,128)} %bitcast.8), calls=%async_computation | async-start | bytes 131072 | tf_op jit(solution)/shard_map/all_to_all | solution.py:493
  22.1 0.6 %copy-start.1 = (f32[112,128]{1,0:T(8,128)}, f32[112,128]{1,0:T(8,128)S(1)}, u32[]{:S(2)}) copy-start(f32[112,128]{1,0:T(8,128)S(1)} %collective-permute-done.even_hbm) | copy-start | bytes 172036
  22.1 0.6 %copy-start.2 = (f32[112,128]{1,0:T(8,128)}, f32[112,128]{1,0:T(8,128)S(1)}, u32[]{:S(2)}) copy-start(f32[112,128]{1,0:T(8,128)S(1)} %collective-permute-done.1.odd_hbm) | copy-start | bytes 172036
  22.1 0.6 %copy-start.3 = (f32[112,128]{1,0:T(8,128)}, f32[112,128]{1,0:T(8,128)S(1)}, u32[]{:S(2)}) copy-start(f32[112,128]{1,0:T(8,128)S(1)} %collective-permute-done.3.cross_hbm) | copy-start | bytes 172036
  22.2 0.6 %copy-start.4 = (f32[112,128]{1,0:T(8,128)}, f32[112,128]{1,0:T(8,128)S(1)}, u32[]{:S(2)}) copy-start(f32[112,128]{1,0:T(8,128)S(1)} %collective-permute-done.2.pair_hbm) | copy-start | bytes 172036
  30.8 0.6 %copy-start = (f32[128,1,128]{2,1,0:T(1,128)}, f32[128,1,128]{2,1,0:T(1,128)S(1)}, u32[]{:S(2)}) copy-start(f32[128,1,128]{2,1,0:T(1,128)S(1)} %all-to-all-done) | copy-start | bytes 196612
